TPU v7x, 256 devices: a whole 4x4x8 slice. The times are simulated.
256 devices in a mesh: dp: 32 (over x, y, core), expert: 8 (over z).
Axes of the slice: x: 4, y: 4, z: 8, core: 2. Of those that a mesh axis runs over, the one named last changes fastest.
Arguments:
- tokens: bfloat16 [1024, 4096], P('expert', 'dp'), may hold values from -6 to 6
- in_signs: int32 [1024, 128], P('expert', 'dp'), may hold values from -2147483648 to 2147483646
- out_signs: int32 [1024, 224], P('expert'), may hold values from -2147483648 to 2147483646
- expert_ids: int32 [1024, 2], P('expert'), may hold values from 0 to 7, all different within a row; in each aligned block of 128 rows (0 to 127, 128 to 255, ...) at most 40 rows name the same one
- route_weight: float32 [1024, 2], P('expert'), may hold values from 0.2 to 1
- cotangent: bfloat16 [1024, 7168], P('expert', 'dp'), may hold values from -6 to 6
- mean_weight: bfloat16 [8, 4096, 7168], P('expert', 'dp'), may hold values from -0.09375 to 0.09375
- rho_weight: bfloat16 [8, 4096, 7168], P('expert', 'dp'), may hold values from -6 to -3
- noise_weight: bfloat16 [8, 4096, 7168], P('expert', 'dp'), may hold values from -4 to 4
Outputs:
- hidden_out: bfloat16 [1024, 7168], P('expert', 'dp')
- grad_tokens: bfloat16 [1024, 4096], P('expert', 'dp')
- grad_mean: bfloat16 [8, 4096, 7168], P('expert', 'dp')
- grad_rho: bfloat16 [8, 4096, 7168], P('expert', 'dp')
Inputs may be any that keep to these rules, and one draw needn't show every extreme that they name: `expert_ids`: each token names 2 different experts. In each aligned block of 128 tokens no expert is named by more than 40 tokens, and in some blocks one expert is named by exactly 40. `in_signs`: bit b of word w, counted from the lowest, is set where the sign of feature 32 * w + b is -1 and clear where it is +1. `out_signs`: bit b of word w, counted from the lowest, is set where the sign of hidden unit 32 * w + b is -1 and clear where it is +1.
All inputs are finite; a program needn't handle non-finite values.
Results may differ from a plain program's by a relative error of at most 0.0071.
Values may be sent and summed in bfloat16 or wider, within the bound.
No kernel may reach another device: no remote copies, remote signals or barrier semaphores. Data moves between devices by JAX's collectives and lax.ppermute only.
A program may use at most 128 MiB of HBM per device.

v0:
```python
import functools

import jax
import jax.numpy as jnp
from jax import lax
from jax.experimental import pallas as pl
from jax.experimental.pallas import tpu as pltpu
from jax.sharding import Mesh, PartitionSpec as P


F32 = jnp.float32
BF16 = jnp.bfloat16
I32 = jnp.int32

EXPERTS = 8
CAP = 40
SLOTS = EXPERTS * CAP
TOK = 128
FEAT = 128
FF = 7168
CHIPS = 16
UNIT = FF // (2 * CHIPS)
WORDS = UNIT // 32
HALF_WORDS = CHIPS * WORDS
WIDE = 256
REST = UNIT - 128
PACK = SLOTS * UNIT // 128
FOLD = PACK - SLOTS
TAIL = SLOTS - FOLD
GROUP = 4 * UNIT
GROUPS = FF // GROUP
PER_STEP = 4


def iota(shape, dim):
    return lax.broadcasted_iota(I32, shape, dim)


def dot(a, b, dims=((1,), (0,))):
    return lax.dot_general(a, b, (dims, ((), ())), preferred_element_type=F32)


def smem():
    return pl.BlockSpec(memory_space=pltpu.SMEM)


def params(*semantics):
    return pltpu.CompilerParams(
        dimension_semantics=semantics or None, vmem_limit_bytes=16 << 20
    )


def cost(flops, nbytes, trans=0):
    return pl.CostEstimate(flops=flops, bytes_accessed=nbytes, transcendentals=trans)


def ranks_of(ids):
    e = iota((EXPERTS, TOK), 0)
    first = ids[0:1, :] == e
    second = ids[1:2, :] == e
    named = jnp.where(first | second, 1.0, 0.0).astype(BF16)
    before = jnp.where(iota((TOK, TOK), 0) < iota((TOK, TOK), 1), 1.0, 0.0).astype(BF16)
    return first, second, dot(named, before)


def slot_match(mask, rank):
    code = jnp.where(mask, rank, -1.0)
    c = iota((CAP, TOK), 0).astype(F32)
    rows = [
        jnp.where(jnp.broadcast_to(code[e : e + 1, :], (CAP, TOK)) == c, 1.0, 0.0)
        for e in range(EXPERTS)
    ]
    return jnp.concatenate(rows, axis=0)


def sign_bits(words, base):
    lane = iota(words.shape, 1)
    picked = jnp.take_along_axis(
        words, base + lax.shift_right_logical(lane, 5), axis=1, mode="promise_in_bounds"
    )
    return (lax.shift_right_logical(picked, lane & 31) & 1) == 1


def flip(bits, x):
    return jnp.where(bits, -x, x)


def fold(second):
    lane = iota((FOLD, 128), 1)
    tail = second[FOLD:, :]
    moved = [pltpu.roll(tail, (REST - 32 * i) % 128, 1) for i in range(3)]
    return jnp.where(lane < REST, second[:FOLD, :], jnp.concatenate(moved, axis=0))


def unfold(q):
    lane = iota((TAIL, 128), 1)
    r = [pltpu.roll(q[TAIL * i : TAIL * (i + 1), :], 32 * (i + 1), 1) for i in range(3)]
    tail = jnp.where(lane < 32, r[0], jnp.where(lane < 64, r[1], r[2]))
    both = jnp.concatenate([q, tail], axis=0)
    return jnp.where(iota((SLOTS, 128), 1) < REST, both, 0.0)


def place(lin):
    return (lin >> 6) & 3, (lin >> 4) & 3, (lin >> 3) & 1


def chunk_at(lin, k, l):
    x, y, c = place(lin)
    east = (x + jnp.where(c == 0, l, k)) & 3
    north = (y + jnp.where(c == 0, k, l)) & 3
    return 4 * east + north


def step_of(lin, q, other):
    x, y, c = place(lin)
    dx = (x - (q >> 2)) & 3
    dy = (y - (q & 3)) & 3
    swapped = (c == 0) == bool(other)
    return jnp.where(swapped, 4 * dx + dy, 4 * dy + dx)


def hop(array, steps, first):
    pairs = []
    for x in range(4):
        for y in range(4):
            for c in range(2):
                along_y = (c == 0) == first
                to_x, to_y = (x, (y + steps) % 4) if along_y else ((x + steps) % 4, y)
                pairs.append(((x * 4 + y) * 2 + c, (to_x * 4 + to_y) * 2 + c))
    return lax.ppermute(array, ("x", "y", "core"), pairs)


def dispatch_body(core, ids, route, tok, tok_o, ins, ins_o, outs, cot, send_ref):
    c = core[0]
    first, second, rank = ranks_of(ids[...])
    match = slot_match(first | second, rank)
    weight = jnp.where(first, route[0:1, :], jnp.where(second, route[1:2, :], 0.0))
    slot_weight = jnp.concatenate(
        [
            jnp.sum(
                match[CAP * e : CAP * (e + 1), :] * weight[e : e + 1, :], axis=1, keepdims=True
            )
            for e in range(EXPERTS)
        ],
        axis=0,
    )
    hot = match.astype(BF16)
    send_ref[:, :FEAT] = dot(hot, tok[...]).astype(BF16)
    send_ref[:, FEAT:WIDE] = dot(hot, tok_o[...]).astype(BF16)
    padded = jnp.concatenate([cot[...], jnp.zeros((WIDE - UNIT, TOK), BF16)], axis=0)
    send_ref[:, WIDE : 2 * WIDE] = (dot(hot, padded, ((1,), (1,))) * slot_weight).astype(BF16)
    i = iota((HALF_WORDS, FF // 32), 0)
    seventh = lax.shift_right_logical(i * 9363, 16)
    source = 2 * WORDS * seventh + WORDS * c + (i - WORDS * seventh)
    half = jnp.where(iota((HALF_WORDS, FF // 32), 1) == source, 1.0, 0.0).astype(BF16)
    small = jnp.concatenate([ins[...], ins_o[...], jnp.zeros((8, TOK), I32)], axis=0)
    for k in range(4):
        low = (lax.shift_right_logical(outs[...], 8 * k) & 255).astype(F32).astype(BF16)
        kept = dot(half, low)
        rest = (lax.shift_right_logical(small, 8 * k) & 255).astype(F32)
        pieces = jnp.concatenate([kept, rest], axis=0).astype(BF16)
        at = 2 * WIDE + 128 * k
        send_ref[:, at : at + 128] = dot(hot, pieces, ((1,), (1,))).astype(BF16)


def delta_body(core, mean, rho, noise, own_ref, oth_ref):
    c = core[0]
    delta = jnp.log(1.0 + jnp.exp(rho[0].astype(F32))) * noise[0].astype(F32)
    lane = iota((FEAT, WIDE), 1)
    for which, x in ((0, mean[0].astype(F32)), (1, delta)):
        for j in range(4):
            start = UNIT * j
            base = start // 128 * 128
            off = start - base
            width = min(GROUP - base, 384)
            window = x[:, base : base + width]
            if off:
                window = pltpu.roll(window, width - off, 1)
            chunk = jnp.where(lane < UNIT, window[:, :WIDE], 0.0).astype(BF16)

            @pl.when(c == j % 2)
            def _():
                own_ref[which, j // 2] = chunk

            @pl.when(c != j % 2)
            def _():
                oth_ref[which, j // 2] = chunk


def forward_part(k, lin, rows, signed, words, weights, y_ref):
    for l in range(4):
        mean, delta = (
            jnp.concatenate([weights[l][w, 0], weights[4 + l][w, 0]], axis=0) for w in range(2)
        )
        m = dot(rows, mean)
        p = dot(signed, delta)
        base = WORDS * chunk_at(lin, k, l)
        y1 = m[:, :128] + flip(sign_bits(words, base), p[:, :128])
        y2 = m[:, 128:] + flip(sign_bits(words, base + 4), p[:, 128:])
        y_ref[l, :SLOTS, :] = y1.astype(BF16)
        y_ref[l, SLOTS:, :] = fold(y2).astype(BF16)


def forward_first(k, lin, got, *refs):
    weights, (y_ref, words_ref, signed_ref) = refs[:8], refs[8:]
    words = jnp.zeros((SLOTS, 128), I32)
    for j in range(4):
        at = 2 * WIDE + 128 * j
        plane = got[:, at : at + 128].astype(F32).astype(I32)
        words = words | lax.shift_left(plane, 8 * j)
    words_ref[...] = words
    for side in range(2):
        bits = sign_bits(words, HALF_WORDS + 4 * side)
        a = got[:, FEAT * side : FEAT * (side + 1)].astype(F32)
        signed_ref[:, FEAT * side : FEAT * (side + 1)] = flip(bits, a).astype(BF16)
    forward_part(k, lin[0], got[:, :WIDE], signed_ref[...], words_ref[...], weights, y_ref)


def forward_next(k, lin, rows, signed, words, *refs):
    forward_part(k, lin[0], rows[...], signed[...], words[...], refs[:8], refs[8])


def halfway_body(p0, r1, r2, r3, q0, q1, q2, q3):
    for l, q in enumerate((q0, q1, q2, q3)):
        total = p0[l].astype(F32) + r1[l].astype(F32)
        total = total + (r2[l].astype(F32) + r3[l].astype(F32))
        q[...] = total.astype(q.dtype)


def middle_body(q0, t1, t2, t3, up, h_ref, dy_ref):
    total = q0[...] + t1[...].astype(F32) + (t2[...].astype(F32) + t3[...].astype(F32))
    ys = (total[:SLOTS, :], unfold(total[SLOTS:, :]))
    ds = []
    for side, y in enumerate(ys):
        gate = jax.nn.sigmoid(y)
        h_ref[:, 128 * side : 128 * (side + 1)] = (y * gate).astype(BF16)
        u = up[:, 128 * side : 128 * (side + 1)].astype(F32)
        ds.append(u * (gate * (1.0 + y * (1.0 - gate))))
    dy_ref[:SLOTS, :] = ds[0].astype(BF16)
    dy_ref[SLOTS:, :] = fold(ds[1]).astype(BF16)


def stack_body(a, b, c, d, out_ref):
    for i, x in enumerate((a, b, c, d)):
        out_ref[i] = x[...]


def gradient_chunk(words, dy, k):
    packed = dy.astype(F32)
    d1 = packed[:SLOTS, :]
    d2 = unfold(packed[SLOTS:, :])
    plain = jnp.concatenate([d1, d2], axis=1).astype(BF16)
    signed = jnp.concatenate(
        [
            flip(sign_bits(words, WORDS * k), d1),
            flip(sign_bits(words, WORDS * k + 4), d2),
        ],
        axis=1,
    ).astype(BF16)
    return plain, signed


def gradient_body(lin, words, rows, v0, v1, v2, v3, *refs):
    own, near = refs[:4], refs[4:8]
    mine_ref, theirs_ref, g_ref, g_away_ref, rows_t, signed_t, sum_m, sum_d = refs[8:]
    step = pl.program_id(0)

    @pl.when(step == 0)
    def _():
        for side in range(2):
            lanes = slice(FEAT * side, FEAT * (side + 1))
            a = rows[:, lanes].astype(F32)
            bits = sign_bits(words[...], HALF_WORDS + 4 * side)
            rows_t[lanes, :] = a.T.astype(BF16)
            signed_t[lanes, :] = flip(bits, a).T.astype(BF16)
        sum_m[...] = jnp.zeros_like(sum_m)
        sum_d[...] = jnp.zeros_like(sum_d)

    plains = []
    signeds = []
    for i in range(PER_STEP):
        dy = jnp.where(
            step < 2,
            jnp.where(step == 0, v0[i], v1[i]),
            jnp.where(step == 2, v2[i], v3[i]),
        )
        plain, signed = gradient_chunk(words[...], dy, chunk_at(lin[0], -step, -i))
        plains.append(plain)
        signeds.append(signed)
        for which, g in ((0, dot(rows_t[...], plain)), (1, dot(signed_t[...], signed))):
            mine_ref[which, i] = g[:FEAT, :].astype(BF16)
            theirs_ref[which, i] = g[FEAT:, :].astype(BF16)
    for which, parts, total in ((0, plains, sum_m), (1, signeds, sum_d)):
        weights = jnp.concatenate(
            [
                jnp.concatenate([w[which, 0] for w in side], axis=1)
                for side in (own, near)
            ],
            axis=0,
        )
        total[...] += dot(jnp.concatenate(parts, axis=1), weights, ((1,), (1,)))

    @pl.when(step == pl.num_programs(0) - 1)
    def _():
        for side, ref in ((0, g_ref), (1, g_away_ref)):
            lanes = slice(FEAT * side, FEAT * (side + 1))
            bits = sign_bits(words[...], HALF_WORDS + 4 * side)
            ref[...] = sum_m[:, lanes] + flip(bits, sum_d[:, lanes])


def slots_body(g, g_near, hidden, send_ref):
    send_ref[:, :FEAT] = (g[...] + g_near[...]).astype(BF16)
    send_ref[:, FEAT:] = hidden[...]


def assemble_body(lin, *refs):
    _, _, c = place(lin[0])
    mine, theirs, (rho, noise, gm_ref, gr_ref) = refs[:4], refs[4:8], refs[8:]

    def laid(which, at):
        out = []
        for i in (at, at + 1):
            for p in range(2):
                out.append(jnp.where(c == p, mine[i][which, 0], theirs[i][which, 0])[:, :UNIT])
        return jnp.concatenate([x.astype(F32) for x in out], axis=1)

    for half in range(PER_STEP // 2):
        lanes = slice(GROUP * half, GROUP * (half + 1))
        gm_ref[0, :, lanes] = laid(0, 2 * half).astype(BF16)
        e = jnp.exp(rho[0, :, lanes].astype(F32))
        factor = noise[0, :, lanes].astype(F32) * (e / (1.0 + e))
        gr_ref[0, :, lanes] = (laid(1, 2 * half) * factor).astype(BF16)


def combine_body(ids, route, got, hidden_ref, tokens_ref):
    first, second, rank = ranks_of(ids[...])
    total = jnp.zeros((WIDE, TOK), F32)
    both = jnp.zeros((SLOTS, TOK), F32)
    for k, mask in enumerate((first, second)):
        match = slot_match(mask, rank)
        both = both + match
        picked = dot(got[:, FEAT:], match.astype(BF16), ((0,), (0,)))
        total = total + picked * route[k : k + 1, :]
    hidden_ref[...] = total[:UNIT, :].astype(BF16)
    tokens_ref[...] = dot(both.astype(BF16), got[:, :FEAT], ((0,), (0,))).astype(BF16)


def whole(*shape):
    return pl.BlockSpec(shape, lambda *_: (0,) * len(shape))


def far_memory(*xs):
    return [pltpu.with_memory_space_constraint(x, pltpu.HBM) for x in xs]


def struct(shape, dtype):
    return jax.ShapeDtypeStruct(shape, dtype)


def on_device(
    tokens, in_signs, out_signs, expert_ids, route_weight, cotangent,
    mean_weight, rho_weight, noise_weight,
):
    mean_weight, rho_weight, noise_weight = far_memory(mean_weight, rho_weight, noise_weight)
    core = lax.axis_index("core").astype(I32).reshape(1)
    lin = lax.axis_index(("x", "y", "core", "expert")).astype(I32).reshape(1)
    swap = [(0, 1), (1, 0)]
    ids = expert_ids.T
    route = route_weight.T
    ins = in_signs.T

    tok_o = lax.ppermute(tokens, "core", swap)
    ins_o = lax.ppermute(ins, "core", swap)

    raw = far_memory(ids, route, tokens)
    raw += [tok_o, *far_memory(ins), ins_o, *far_memory(out_signs.T, cotangent.T)]
    send = pl.pallas_call(
        dispatch_body,
        grid=(1,),
        in_specs=[smem()] + [whole(*x.shape) for x in raw],
        out_specs=whole(SLOTS, 4 * WIDE),
        out_shape=struct((SLOTS, 4 * WIDE), BF16),
        compiler_params=params("arbitrary"),
        cost_estimate=cost(400_000_000, 1 << 20),
        name="dispatch",
    )(core, *raw)

    def exchange(x):
        wide = x.reshape(EXPERTS, CAP, x.shape[1])
        got = lax.all_to_all(wide, "expert", split_axis=0, concat_axis=0, tiled=True)
        return got.reshape(x.shape)

    got = exchange(send)

    late, _ = lax.optimization_barrier((core, send))
    block = pl.BlockSpec((1, FEAT, GROUP), lambda g: (0, 0, g))
    pair = pl.BlockSpec((2, 2, FEAT, WIDE), lambda g: (0, g, 0, 0))
    own, away = pl.pallas_call(
        delta_body,
        grid=(GROUPS,),
        in_specs=[smem(), block, block, block],
        out_specs=(pair, pair),
        out_shape=(pltpu.HBM((2, CHIPS, FEAT, WIDE), BF16),) * 2,
        compiler_params=params("arbitrary"),
        cost_estimate=cost(2_000_000_000, 10 << 20, 2 * FEAT * FF),
        name="delta",
    )(late, mean_weight, rho_weight, noise_weight)
    near = lax.ppermute(away, "core", swap)

    steps = CHIPS // PER_STEP
    table = whole(SLOTS, 128)
    rows_spec = pl.BlockSpec((SLOTS, WIDE), lambda *_: (0, 0))
    quad = struct((4, PACK, 128), BF16)
    quad_spec = whole(4, PACK, 128)
    lone_spec = whole(PACK, 128)

    def picked(index):
        return pl.BlockSpec(
            (2, 1, FEAT, WIDE), lambda i, lin: (0, index(lin[0], i), 0, 0)
        )

    def grid_spec(n, ins, outs, scratch=()):
        return pltpu.PrefetchScalarGridSpec(
            num_scalar_prefetch=1, grid=(n,), in_specs=ins, out_specs=outs,
            scratch_shapes=scratch,
        )

    sent = [None] * 4
    words = signed = None
    for k in (1, 3, 2, 0):
        chunks = [
            picked(lambda lin, i, k=k, l=l: chunk_at(lin, k, l)) for l in range(4)
        ] * 2
        if words is None:
            sent[k], words, signed = pl.pallas_call(
                functools.partial(forward_first, k),
                grid_spec=grid_spec(
                    1, [whole(SLOTS, 4 * WIDE), *chunks], (quad_spec, table, rows_spec)
                ),
                out_shape=(quad, struct((SLOTS, 128), I32), struct((SLOTS, WIDE), BF16)),
                compiler_params=params("arbitrary"),
                cost_estimate=cost(600_000_000, 2 << 20),
            )(lin, got, *[own] * 4, *[near] * 4)
        else:
            sent[k] = pl.pallas_call(
                functools.partial(forward_next, k),
                grid_spec=grid_spec(1, [rows_spec, rows_spec, table, *chunks], quad_spec),
                out_shape=quad,
                compiler_params=params("arbitrary"),
                cost_estimate=cost(600_000_000, 2 << 20),
            )(lin, got, signed, words, *[own] * 4, *[near] * 4)
    parts = [sent[0]] + [hop(sent[k], k, True) for k in (1, 2, 3)]
    lone = struct((PACK, 128), BF16)
    kept, *passed = pl.pallas_call(
        halfway_body,
        grid=(1,),
        in_specs=[quad_spec] * 4,
        out_specs=(lone_spec,) * 4,
        out_shape=(struct((PACK, 128), F32), lone, lone, lone),
        compiler_params=params("arbitrary"),
        cost_estimate=cost(200_000_000, 3 << 20),
        name="halfway",
    )(*parts)
    passed = [hop(passed[l - 1], l, False) for l in (1, 2, 3)]
    hidden, dy = pl.pallas_call(
        middle_body,
        grid=(1,),
        in_specs=[lone_spec] * 4 + [pl.BlockSpec((SLOTS, WIDE), lambda *_: (0, 1))],
        out_specs=(whole(SLOTS, WIDE), lone_spec),
        out_shape=(struct((SLOTS, WIDE), BF16), lone),
        compiler_params=params("arbitrary"),
        cost_estimate=cost(200_000_000, 1 << 20),
        name="middle",
    )(kept, *passed, got)
    stack = pl.pallas_call(
        stack_body,
        grid=(1,),
        in_specs=[lone_spec] * 4,
        out_specs=quad_spec,
        out_shape=quad,
        compiler_params=params("arbitrary"),
        cost_estimate=cost(100_000_000, 1 << 20),
        name="stack",
    )(dy, *[hop(dy, l, False) for l in (1, 2, 3)])
    dys = [stack] + [hop(stack, k, True) for k in (1, 2, 3)]

    sums = whole(SLOTS, FEAT)
    side = pltpu.HBM((2, CHIPS, FEAT, WIDE), BF16)
    weights = pl.BlockSpec((2, PER_STEP, FEAT, WIDE), lambda k, lin: (0, k, 0, 0))
    chunks = [picked(lambda lin, i, l=l: chunk_at(lin, -i, -l)) for l in range(4)] * 2
    mine, theirs, g, g_away = pl.pallas_call(
        gradient_body,
        grid_spec=grid_spec(
            steps,
            [table, rows_spec] + [quad_spec] * 4 + chunks,
            (weights, weights, sums, sums),
            [pltpu.VMEM((WIDE, SLOTS), BF16)] * 2 + [pltpu.VMEM((SLOTS, WIDE), F32)] * 2,
        ),
        out_shape=(side, side, struct((SLOTS, FEAT), F32), struct((SLOTS, FEAT), F32)),
        compiler_params=params("arbitrary"),
        cost_estimate=cost(5_000_000_000, 12 << 20),
        name="backward",
    )(lin, words, got, *dys, *[own] * 4, *[near] * 4)
    g_near = lax.ppermute(g_away, "core", swap)
    theirs, _ = lax.optimization_barrier((theirs, g_near))
    theirs = lax.ppermute(theirs, "core", swap)
    send = pl.pallas_call(
        slots_body,
        grid=(1,),
        in_specs=[sums, sums, whole(SLOTS, WIDE)],
        out_specs=whole(SLOTS, FEAT + WIDE),
        out_shape=struct((SLOTS, FEAT + WIDE), BF16),
        compiler_params=params("arbitrary"),
        cost_estimate=cost(100_000_000, 1 << 20),
        name="slots",
    )(g, g_near, hidden)
    back = exchange(send)
    late, _ = lax.optimization_barrier((lin, send))
    wide = pl.BlockSpec((1, FEAT, FF // steps), lambda g, lin: (0, 0, g))
    laid = [
        picked(lambda lin, i, l=l, other=other: step_of(lin, 4 * i + l, other))
        for other in range(2)
        for l in range(4)
    ]
    grad_mean, grad_rho = pl.pallas_call(
        assemble_body,
        grid_spec=grid_spec(steps, [*laid, wide, wide], (wide, wide)),
        out_shape=(struct((1, FEAT, FF), BF16),) * 2,
        compiler_params=params("arbitrary"),
        cost_estimate=cost(3_000_000_000, 12 << 20, FEAT * FF),
        name="assemble",
    )(late, *[mine] * 4, *[theirs] * 4, rho_weight, noise_weight)

    hidden_out, grad_tokens = pl.pallas_call(
        combine_body,
        grid=(1,),
        in_specs=[whole(2, TOK), whole(2, TOK), whole(SLOTS, FEAT + WIDE)],
        out_specs=(whole(UNIT, TOK), whole(TOK, FEAT)),
        out_shape=(struct((UNIT, TOK), BF16), struct((TOK, FEAT), BF16)),
        compiler_params=params("arbitrary"),
        cost_estimate=cost(200_000_000, 1 << 19),
        name="combine",
    )(*far_memory(ids, route), back)
    return hidden_out.T, grad_tokens, grad_mean, grad_rho


def solution(mesh):
    fine = Mesh(mesh.devices.reshape(4, 4, 2, 8), ("x", "y", "core", "expert"))
    dp = ("x", "y", "core")
    in_specs = (
        P("expert", dp),
        P("expert", dp),
        P("expert", None),
        P("expert", None),
        P("expert", None),
        P("expert", dp),
        P("expert", dp, None),
        P("expert", dp, None),
        P("expert", dp, None),
    )
    out_specs = (
        P("expert", dp),
        P("expert", dp),
        P("expert", dp, None),
        P("expert", dp, None),
    )

    return jax.shard_map(
        on_device, mesh=fine, in_specs=in_specs, out_specs=out_specs, check_vma=False
    )
```

profile of v0, /device:TPU:1, one launch (start us, length us, event | category | flops | bytes accessed | tf_op | source)
XLA Modules:
  0.0 148.5 jit_solution(4526223729017407405)
XLA Ops:
  0.6 3.3 %collective-permute-start = (bf16[128,128]{1,0:T(8,128)(2,1)}, bf16[128,128]{1,0:T(8,128)(2,1)S(1)}, u32[]{:S(2)}, u32[]{:S(2)}) collective-permute-start(bf16[128,128]{1,0:T(8,128)(2,1)} %tok.1), channel_id=1, source_target_pairs={{0,8},{8,0},{1,9},{9,1},{2,10},{10,2},{3,11},{11,3},{4,12},{12,4},... | collective-permute-start | bytes 98312 | tf_op jit(solution)/shard_map/ppermute | solution.py:372
  4.0 1.3 collective-permute-done.1.ins_o
  5.3 2.6 %dispatch.1 = bf16[320,1024]{1,0:T(8,128)(2,1)} custom-call(s32[1]{0:T(128)} %bitcast.3.core, s32[2,128]{1,0:T(2,128)} %bitcast.23, f32[2,128]{1,0:T(2,128)} %bitcast.25, bf16[128,128]{1,0:T(8,128)(2,1)} %tok.1, bf16[128,128]{1,0:T(8,128)(2,1)S(1)} %collective-permute-done.tok_o, s32[4,128]{1,0:T(4,128)} %bitcast.22, ...), custom_call_target="tpu_custom_call" | custom-call | flops 400000000 | bytes 1048576 | tf_op jit(solution)/shard_map/dispatch/pallas_call | solution.py:377
  7.9 10.0 %delta.1 = (bf16[2,16,128,256]{3,2,1,0:T(8,128)(2,1)}, bf16[2,16,128,256]{3,2,1,0:T(8,128)(2,1)}) custom-call(s32[1]{0:T(128)} %bitcast.3.core, bf16[1,128,7168]{2,1,0:T(8,128)(2,1)} %mean.1, bf16[1,128,7168]{2,1,0:T(8,128)(2,1)} %refs_8_.1, bf16[1,128,7168]{2,1,0:T(8,128)(2,1)} %refs_9_.1), custom_call_target="tpu_custom_call" | custom-call | flops 2000000000 | bytes 10485760 | tf_op jit(solution)/shard_map/delta/pallas_call | solution.py:398
  18.0 6.5 %all-to-all-start = ((bf16[8,40,1024]{2,1,0:T(8,128)(2,1)}), bf16[8,40,1024]{2,1,0:T(8,128)(2,1)S(1)}, u32[]{:S(2)}, u32[]{:S(2)}) async-start(bf16[8,40,1024]{2,1,0:T(8,128)(2,1)} %bitcast.7), calls=%async_computation | async-start | bytes 1310720 | tf_op jit(solution)/shard_map/all_to_all | solution.py:390
  24.5 20.8 %all-to-all-done = bf16[8,40,1024]{2,1,0:T(8,128)(2,1)S(1)} async-done(((bf16[8,40,1024]{2,1,0:T(8,128)(2,1)}), bf16[8,40,1024]{2,1,0:T(8,128)(2,1)S(1)}, u32[]{:S(2)}, u32[]{:S(2)}) %all-to-all-start) | async-done | bytes 655392 | tf_op jit(solution)/shard_map/all_to_all | solution.py:390
  45.2 1.6 %copy-done = bf16[2,16,128,256]{3,2,1,0:T(8,128)(2,1)S(1)} copy-done((bf16[2,16,128,256]{3,2,1,0:T(8,128)(2,1)S(1)}, bf16[2,16,128,256]{3,2,1,0:T(8,128)(2,1)}, u32[]{:S(2)}) %copy-start) | copy-done | bytes 2097176
  46.8 0.8 shard_map.120
  48.3 2.8 %collective-permute-start.4 = (bf16[4,560,128]{2,1,0:T(8,128)(2,1)S(1)}, bf16[4,560,128]{2,1,0:T(8,128)(2,1)S(1)}, u32[]{:S(2)}, u32[]{:S(2)}) collective-permute-start(bf16[4,560,128]{2,1,0:T(8,128)(2,1)S(1)} %shard_map.122), channel_id=1, source_target_pairs={{0,32},{8,136},{16,48},{24,152},{32,0},{40,168},{48,16},{56,184},{... | collective-permute-start | bytes 1720328 | tf_op jit(solution)/shard_map/ppermute | solution.py:130
  51.7 0.9 collective-permute-start.5
  53.9 4.8 %collective-permute-done.4.r2 = bf16[4,560,128]{2,1,0:T(8,128)(2,1)S(1)} collective-permute-done((bf16[4,560,128]{2,1,0:T(8,128)(2,1)S(1)}, bf16[4,560,128]{2,1,0:T(8,128)(2,1)S(1)}, u32[]{:S(2)}, u32[]{:S(2)}) %collective-permute-start.4) | collective-permute-done | bytes 573472 | tf_op jit(solution)/shard_map/ppermute | solution.py:130
  58.7 6.2 %collective-permute-done.5.r3 = bf16[4,560,128]{2,1,0:T(8,128)(2,1)S(1)} collective-permute-done((bf16[4,560,128]{2,1,0:T(8,128)(2,1)S(1)}, bf16[4,560,128]{2,1,0:T(8,128)(2,1)S(1)}, u32[]{:S(2)}, u32[]{:S(2)}) %collective-permute-start.5) | collective-permute-done | bytes 573472 | tf_op jit(solution)/shard_map/ppermute | solution.py:130
  65.3 1.4 collective-permute-start.6
  66.6 2.6 %collective-permute-start.7 = (bf16[560,128]{1,0:T(8,128)(2,1)S(1)}, bf16[560,128]{1,0:T(8,128)(2,1)S(1)}, u32[]{:S(2)}, u32[]{:S(2)}) collective-permute-start(bf16[560,128]{1,0:T(8,128)(2,1)S(1)} %get-tuple-element.34), channel_id=1, source_target_pairs={{0,128},{8,40},{16,144},{24,56},{32,160},{40,8},{48,176},{56,24},{... | collective-permute-start | bytes 430088 | tf_op jit(solution)/shard_map/ppermute | solution.py:130
  69.3 1.1 collective-permute-start.8
  70.6 2.7 %collective-permute-done.7.t2 = bf16[560,128]{1,0:T(8,128)(2,1)S(1)} collective-permute-done((bf16[560,128]{1,0:T(8,128)(2,1)S(1)}, bf16[560,128]{1,0:T(8,128)(2,1)S(1)}, u32[]{:S(2)}, u32[]{:S(2)}) %collective-permute-start.7) | collective-permute-done | bytes 143392 | tf_op jit(solution)/shard_map/ppermute | solution.py:130
  73.5 2.3 %collective-permute-start.11 = (bf16[560,128]{1,0:T(8,128)(2,1)S(1)}, bf16[560,128]{1,0:T(8,128)(2,1)S(1)}, u32[]{:S(2)}, u32[]{:S(2)}) collective-permute-start(bf16[560,128]{1,0:T(8,128)(2,1)S(1)} %get-tuple-element.36.a), channel_id=1, source_target_pairs={{0,192},{8,56},{16,208},{24,8},{32,224},{40,24},{48,240},{56,40},{... | collective-permute-start | bytes 430088 | tf_op jit(solution)/shard_map/ppermute | solution.py:130
  76.8 2.6 %collective-permute-done.11.d = bf16[560,128]{1,0:T(8,128)(2,1)S(1)} collective-permute-done((bf16[560,128]{1,0:T(8,128)(2,1)S(1)}, bf16[560,128]{1,0:T(8,128)(2,1)S(1)}, u32[]{:S(2)}, u32[]{:S(2)}) %collective-permute-start.11) | collective-permute-done | bytes 143392 | tf_op jit(solution)/shard_map/ppermute | solution.py:130
  79.4 2.0 %collective-permute-done.10.c = bf16[560,128]{1,0:T(8,128)(2,1)S(1)} collective-permute-done((bf16[560,128]{1,0:T(8,128)(2,1)S(1)}, bf16[560,128]{1,0:T(8,128)(2,1)S(1)}, u32[]{:S(2)}, u32[]{:S(2)}) %collective-permute-start.10) | collective-permute-done | bytes 143392 | tf_op jit(solution)/shard_map/ppermute | solution.py:130
  81.4 1.4 collective-permute-done.9.b
  82.8 2.7 %collective-permute-start.14 = (bf16[4,560,128]{2,1,0:T(8,128)(2,1)S(1)}, bf16[4,560,128]{2,1,0:T(8,128)(2,1)S(1)}, u32[]{:S(2)}, u32[]{:S(2)}) collective-permute-start(bf16[4,560,128]{2,1,0:T(8,128)(2,1)S(1)} %stack.1.v0), channel_id=1, source_target_pairs={{0,48},{8,200},{16,0},{24,216},{32,16},{40,232},{48,32},{56,248},{... | collective-permute-start | bytes 1720328 | tf_op jit(solution)/shard_map/ppermute | solution.py:130
  86.7 11.7 %collective-permute-done.14.v3 = bf16[4,560,128]{2,1,0:T(8,128)(2,1)S(1)} collective-permute-done((bf16[4,560,128]{2,1,0:T(8,128)(2,1)S(1)}, bf16[4,560,128]{2,1,0:T(8,128)(2,1)S(1)}, u32[]{:S(2)}, u32[]{:S(2)}) %collective-permute-start.14) | collective-permute-done | bytes 573472 | tf_op jit(solution)/shard_map/ppermute | solution.py:130
  98.4 3.7 %collective-permute-done.12.v1 = bf16[4,560,128]{2,1,0:T(8,128)(2,1)S(1)} collective-permute-done((bf16[4,560,128]{2,1,0:T(8,128)(2,1)S(1)}, bf16[4,560,128]{2,1,0:T(8,128)(2,1)S(1)}, u32[]{:S(2)}, u32[]{:S(2)}) %collective-permute-start.12) | collective-permute-done | bytes 573472 | tf_op jit(solution)/shard_map/ppermute | solution.py:130
  102.1 9.0 %backward.1 = (bf16[2,16,128,256]{3,2,1,0:T(8,128)(2,1)}, bf16[2,16,128,256]{3,2,1,0:T(8,128)(2,1)}, f32[320,128]{1,0:T(8,128)S(1)}, f32[320,128]{1,0:T(8,128)S(1)}) custom-call(s32[1]{0:T(128)} %bitcast.2.lin, s32[320,128]{1,0:T(8,128)S(1)} %get-tuple-element.29.words, bf16[320,1024]{1,0:T(8,128)(2,1)S(1)} %bitcast.17, bf16[4,560,128]{2,1,0:T(8,128)(2,1)S(1)} %stack.1.v0, ...), custom_call_target="tpu_custom_call" | custom-call | flops 5000000000 | bytes 12582912 | tf_op jit(solution)/shard_map/backward/pallas_call | solution.py:491
  111.0 5.4 %collective-permute-start.15 = (f32[320,128]{1,0:T(8,128)S(1)}, f32[320,128]{1,0:T(8,128)S(1)}, u32[]{:S(2)}, u32[]{:S(2)}) collective-permute-start(f32[320,128]{1,0:T(8,128)S(1)} %get-tuple-element.38), channel_id=1, source_target_pairs={{0,8},{8,0},{1,9},{9,1},{2,10},{10,2},{3,11},{11,3},{4,12},{12,4},... | collective-permute-start | bytes 491528 | tf_op jit(solution)/shard_map/ppermute | solution.py:504
  116.5 1.0 collective-permute-done.15.g_near
  117.9 0.7 slots.1
  118.6 9.2 %all-to-all-start.1 = ((bf16[8,40,384]{2,1,0:T(8,128)(2,1)}), bf16[8,40,384]{2,1,0:T(8,128)(2,1)S(1)}, u32[]{:S(2)}, u32[]{:S(2)}) async-start(bf16[8,40,384]{2,1,0:T(8,128)(2,1)} %bitcast.9), calls=%async_computation.1 | async-start | bytes 491520 | tf_op jit(solution)/shard_map/all_to_all | solution.py:390
  127.8 11.9 %all-to-all-done.1 = bf16[8,40,384]{2,1,0:T(8,128)(2,1)S(1)} async-done(((bf16[8,40,384]{2,1,0:T(8,128)(2,1)}), bf16[8,40,384]{2,1,0:T(8,128)(2,1)S(1)}, u32[]{:S(2)}, u32[]{:S(2)}) %all-to-all-start.1) | async-done | bytes 245792 | tf_op jit(solution)/shard_map/all_to_all | solution.py:390
  139.6 1.7 %combine.1 = (bf16[224,128]{1,0:T(8,128)(2,1)}, bf16[128,128]{1,0:T(8,128)(2,1)}) custom-call(s32[2,128]{1,0:T(2,128)} %bitcast.24, f32[2,128]{1,0:T(2,128)} %bitcast.26, bf16[320,384]{1,0:T(8,128)(2,1)S(1)} %bitcast.18), custom_call_target="tpu_custom_call" | custom-call | flops 200000000 | bytes 524288 | tf_op jit(solution)/shard_map/combine/pallas_call | solution.py:534
  141.4 1.6 %copy-done.2 = bf16[2,16,128,256]{3,2,1,0:T(8,128)(2,1)S(1)} copy-done((bf16[2,16,128,256]{3,2,1,0:T(8,128)(2,1)S(1)}, bf16[2,16,128,256]{3,2,1,0:T(8,128)(2,1)}, u32[]{:S(2)}) %copy-start.2) | copy-done | bytes 2097176
  142.9 5.5 %assemble.1 = (bf16[1,128,7168]{2,1,0:T(8,128)(2,1)}, bf16[1,128,7168]{2,1,0:T(8,128)(2,1)}) custom-call(s32[1]{0:T(128)} %bitcast.2.lin, bf16[2,16,128,256]{3,2,1,0:T(8,128)(2,1)S(1)} %copy-done.2, bf16[2,16,128,256]{3,2,1,0:T(8,128)(2,1)S(1)} %copy-done.2, bf16[2,16,128,256]{3,2,1,0:T(8,128)(2,1)S(1)} %copy-done.2, ...), custom_call_target="tpu_custom_call" | custom-call | flops 3000000000 | bytes 12582912 | tf_op jit(solution)/shard_map/assemble/pallas_call | solution.py:525
  (25 shorter events, 6.0 us)
Async XLA Ops:
  0.6 4.7 %collective-permute-start = (bf16[128,128]{1,0:T(8,128)(2,1)}, bf16[128,128]{1,0:T(8,128)(2,1)S(1)}, u32[]{:S(2)}, u32[]{:S(2)}) collective-permute-start(bf16[128,128]{1,0:T(8,128)(2,1)} %tok.1), channel_id=1, source_target_pairs={{0,8},{8,0},{1,9},{9,1},{2,10},{10,2},{3,11},{11,3},{4,12},{12,4},... | collective-permute-start | bytes 98312 | tf_op jit(solution)/shard_map/ppermute | solution.py:372
  3.9 1.4 collective-permute-start.1
  17.8 27.4 %collective-permute-start.2 = (bf16[2,16,128,256]{3,2,1,0:T(8,128)(2,1)}, bf16[2,16,128,256]{3,2,1,0:T(8,128)(2,1)S(1)}, u32[]{:S(2)}, u32[]{:S(2)}) collective-permute-start(bf16[2,16,128,256]{3,2,1,0:T(8,128)(2,1)} %get-tuple-element.28), channel_id=1, source_target_pairs={{0,8},{8,0},{1,9},{9,1},{2,10},{10,2},{3,11},{11,3},{4,12},{12,4},... | collective-permute-start | bytes 6291464 | tf_op jit(solution)/shard_map/ppermute | solution.py:408
  18.0 27.2 %all-to-all-start = ((bf16[8,40,1024]{2,1,0:T(8,128)(2,1)}), bf16[8,40,1024]{2,1,0:T(8,128)(2,1)S(1)}, u32[]{:S(2)}, u32[]{:S(2)}) async-start(bf16[8,40,1024]{2,1,0:T(8,128)(2,1)} %bitcast.7), calls=%async_computation | async-start | bytes 1310720 | tf_op jit(solution)/shard_map/all_to_all | solution.py:390
  45.2 1.6 %copy-start = (bf16[2,16,128,256]{3,2,1,0:T(8,128)(2,1)S(1)}, bf16[2,16,128,256]{3,2,1,0:T(8,128)(2,1)}, u32[]{:S(2)}) copy-start(bf16[2,16,128,256]{3,2,1,0:T(8,128)(2,1)} %get-tuple-element.27.refs_0_.refs_1_.refs_2_.refs_3_) | copy-start | bytes 6291460
  48.3 10.5 %collective-permute-start.4 = (bf16[4,560,128]{2,1,0:T(8,128)(2,1)S(1)}, bf16[4,560,128]{2,1,0:T(8,128)(2,1)S(1)}, u32[]{:S(2)}, u32[]{:S(2)}) collective-permute-start(bf16[4,560,128]{2,1,0:T(8,128)(2,1)S(1)} %shard_map.122), channel_id=1, source_target_pairs={{0,32},{8,136},{16,48},{24,152},{32,0},{40,168},{48,16},{56,184},{... | collective-permute-start | bytes 1720328 | tf_op jit(solution)/shard_map/ppermute | solution.py:130
  51.7 13.2 %collective-permute-start.5 = (bf16[4,560,128]{2,1,0:T(8,128)(2,1)S(1)}, bf16[4,560,128]{2,1,0:T(8,128)(2,1)S(1)}, u32[]{:S(2)}, u32[]{:S(2)}) collective-permute-start(bf16[4,560,128]{2,1,0:T(8,128)(2,1)S(1)} %shard_map.123), channel_id=1, source_target_pairs={{0,48},{8,200},{16,0},{24,216},{32,16},{40,232},{48,32},{56,248},{... | collective-permute-start | bytes 1720328 | tf_op jit(solution)/shard_map/ppermute | solution.py:130
  52.7 12.3 %collective-permute-start.3 = (bf16[4,560,128]{2,1,0:T(8,128)(2,1)S(1)}, bf16[4,560,128]{2,1,0:T(8,128)(2,1)S(1)}, u32[]{:S(2)}, u32[]{:S(2)}) collective-permute-start(bf16[4,560,128]{2,1,0:T(8,128)(2,1)S(1)} %get-tuple-element.31), channel_id=1, source_target_pairs={{0,16},{8,72},{16,32},{24,88},{32,48},{40,104},{48,0},{56,120},{64... | collective-permute-start | bytes 1720328 | tf_op jit(solution)/shard_map/ppermute | solution.py:130
  53.9 48.2 %copy-start.1 = (bf16[2,16,128,256]{3,2,1,0:T(8,128)(2,1)S(1)}, bf16[2,16,128,256]{3,2,1,0:T(8,128)(2,1)}, u32[]{:S(2)}) copy-start(bf16[2,16,128,256]{3,2,1,0:T(8,128)(2,1)} %get-tuple-element.27.refs_0_.refs_1_.refs_2_.refs_3_) | copy-start | bytes 6291460
  65.3 5.3 %collective-permute-start.6 = (bf16[560,128]{1,0:T(8,128)(2,1)S(1)}, bf16[560,128]{1,0:T(8,128)(2,1)S(1)}, u32[]{:S(2)}, u32[]{:S(2)}) collective-permute-start(bf16[560,128]{1,0:T(8,128)(2,1)S(1)} %get-tuple-element.33), channel_id=1, source_target_pairs={{0,64},{8,24},{16,80},{24,40},{32,96},{40,56},{48,112},{56,8},{64,... | collective-permute-start | bytes 430088 | tf_op jit(solution)/shard_map/ppermute | solution.py:130
  66.6 6.6 %collective-permute-start.7 = (bf16[560,128]{1,0:T(8,128)(2,1)S(1)}, bf16[560,128]{1,0:T(8,128)(2,1)S(1)}, u32[]{:S(2)}, u32[]{:S(2)}) collective-permute-start(bf16[560,128]{1,0:T(8,128)(2,1)S(1)} %get-tuple-element.34), channel_id=1, source_target_pairs={{0,128},{8,40},{16,144},{24,56},{32,160},{40,8},{48,176},{56,24},{... | collective-permute-start | bytes 430088 | tf_op jit(solution)/shard_map/ppermute | solution.py:130
  69.3 4.0 %collective-permute-start.8 = (bf16[560,128]{1,0:T(8,128)(2,1)S(1)}, bf16[560,128]{1,0:T(8,128)(2,1)S(1)}, u32[]{:S(2)}, u32[]{:S(2)}) collective-permute-start(bf16[560,128]{1,0:T(8,128)(2,1)S(1)} %get-tuple-element.35), channel_id=1, source_target_pairs={{0,192},{8,56},{16,208},{24,8},{32,224},{40,24},{48,240},{56,40},{... | collective-permute-start | bytes 430088 | tf_op jit(solution)/shard_map/ppermute | solution.py:130
  73.5 5.9 %collective-permute-start.11 = (bf16[560,128]{1,0:T(8,128)(2,1)S(1)}, bf16[560,128]{1,0:T(8,128)(2,1)S(1)}, u32[]{:S(2)}, u32[]{:S(2)}) collective-permute-start(bf16[560,128]{1,0:T(8,128)(2,1)S(1)} %get-tuple-element.36.a), channel_id=1, source_target_pairs={{0,192},{8,56},{16,208},{24,8},{32,224},{40,24},{48,240},{56,40},{... | collective-permute-start | bytes 430088 | tf_op jit(solution)/shard_map/ppermute | solution.py:130
  75.8 5.6 %collective-permute-start.10 = (bf16[560,128]{1,0:T(8,128)(2,1)S(1)}, bf16[560,128]{1,0:T(8,128)(2,1)S(1)}, u32[]{:S(2)}, u32[]{:S(2)}) collective-permute-start(bf16[560,128]{1,0:T(8,128)(2,1)S(1)} %get-tuple-element.36.a), channel_id=1, source_target_pairs={{0,128},{8,40},{16,144},{24,56},{32,160},{40,8},{48,176},{56,24},{... | collective-permute-start | bytes 430088 | tf_op jit(solution)/shard_map/ppermute | solution.py:130
  76.3 6.5 %collective-permute-start.9 = (bf16[560,128]{1,0:T(8,128)(2,1)S(1)}, bf16[560,128]{1,0:T(8,128)(2,1)S(1)}, u32[]{:S(2)}, u32[]{:S(2)}) collective-permute-start(bf16[560,128]{1,0:T(8,128)(2,1)S(1)} %get-tuple-element.36.a), channel_id=1, source_target_pairs={{0,64},{8,24},{16,80},{24,40},{32,96},{40,56},{48,112},{56,8},{64,... | collective-permute-start | bytes 430088 | tf_op jit(solution)/shard_map/ppermute | solution.py:130
  82.8 15.5 %collective-permute-start.14 = (bf16[4,560,128]{2,1,0:T(8,128)(2,1)S(1)}, bf16[4,560,128]{2,1,0:T(8,128)(2,1)S(1)}, u32[]{:S(2)}, u32[]{:S(2)}) collective-permute-start(bf16[4,560,128]{2,1,0:T(8,128)(2,1)S(1)} %stack.1.v0), channel_id=1, source_target_pairs={{0,48},{8,200},{16,0},{24,216},{32,16},{40,232},{48,32},{56,248},{... | collective-permute-start | bytes 1720328 | tf_op jit(solution)/shard_map/ppermute | solution.py:130
  85.6 12.8 %collective-permute-start.13 = (bf16[4,560,128]{2,1,0:T(8,128)(2,1)S(1)}, bf16[4,560,128]{2,1,0:T(8,128)(2,1)S(1)}, u32[]{:S(2)}, u32[]{:S(2)}) collective-permute-start(bf16[4,560,128]{2,1,0:T(8,128)(2,1)S(1)} %stack.1.v0), channel_id=1, source_target_pairs={{0,32},{8,136},{16,48},{24,152},{32,0},{40,168},{48,16},{56,184},{... | collective-permute-start | bytes 1720328 | tf_op jit(solution)/shard_map/ppermute | solution.py:130
  86.1 15.9 %collective-permute-start.12 = (bf16[4,560,128]{2,1,0:T(8,128)(2,1)S(1)}, bf16[4,560,128]{2,1,0:T(8,128)(2,1)S(1)}, u32[]{:S(2)}, u32[]{:S(2)}) collective-permute-start(bf16[4,560,128]{2,1,0:T(8,128)(2,1)S(1)} %stack.1.v0), channel_id=1, source_target_pairs={{0,16},{8,72},{16,32},{24,88},{32,48},{40,104},{48,0},{56,120},{64... | collective-permute-start | bytes 1720328 | tf_op jit(solution)/shard_map/ppermute | solution.py:130
  111.0 6.4 %collective-permute-start.15 = (f32[320,128]{1,0:T(8,128)S(1)}, f32[320,128]{1,0:T(8,128)S(1)}, u32[]{:S(2)}, u32[]{:S(2)}) collective-permute-start(f32[320,128]{1,0:T(8,128)S(1)} %get-tuple-element.38), channel_id=1, source_target_pairs={{0,8},{8,0},{1,9},{9,1},{2,10},{10,2},{3,11},{11,3},{4,12},{12,4},... | collective-permute-start | bytes 491528 | tf_op jit(solution)/shard_map/ppermute | solution.py:504
  117.5 23.9 %collective-permute-start.16 = (bf16[2,16,128,256]{3,2,1,0:T(8,128)(2,1)}, bf16[2,16,128,256]{3,2,1,0:T(8,128)(2,1)S(1)}, u32[]{:S(2)}, u32[]{:S(2)}) collective-permute-start(bf16[2,16,128,256]{3,2,1,0:T(8,128)(2,1)} %get-tuple-element.45), channel_id=1, source_target_pairs={{0,8},{8,0},{1,9},{9,1},{2,10},{10,2},{3,11},{11,3},{4,12},{12,4},... | collective-permute-start | bytes 6291464 | tf_op jit(solution)/shard_map/ppermute | solution.py:506
  118.6 21.0 %all-to-all-start.1 = ((bf16[8,40,384]{2,1,0:T(8,128)(2,1)}), bf16[8,40,384]{2,1,0:T(8,128)(2,1)S(1)}, u32[]{:S(2)}, u32[]{:S(2)}) async-start(bf16[8,40,384]{2,1,0:T(8,128)(2,1)} %bitcast.9), calls=%async_computation.1 | async-start | bytes 491520 | tf_op jit(solution)/shard_map/all_to_all | solution.py:390
  141.4 1.6 %copy-start.2 = (bf16[2,16,128,256]{3,2,1,0:T(8,128)(2,1)S(1)}, bf16[2,16,128,256]{3,2,1,0:T(8,128)(2,1)}, u32[]{:S(2)}) copy-start(bf16[2,16,128,256]{3,2,1,0:T(8,128)(2,1)} %get-tuple-element.43.refs_0_.refs_1_.refs_2_.refs_3_) | copy-start | bytes 6291460
where the time goes:
time: 149 us; the launch traced here: 148 us
  waiting for transfers between devices  70.4 us (47%)
  starting transfers between devices  41.5 us (28%)
  Pallas kernels  32.7 us (22%)
  local copies, waits for them, and re-layouts  3.19 us (2%)
    ppermute x12, waiting for transfers between devices, hop(): return lax.ppermute(array, ('x', 'y', 'core'), pairs)  35.5 us
    all_to_all x2, waiting for transfers between devices, exchange(): lax.all_to_all(wide, 'expert', split_axis=0, concat_axis=0, tiled=True)  32.6 us
    ppermute x12, starting transfers between devices, hop(): return lax.ppermute(array, ('x', 'y', 'core'), pairs)  16.5 us
    all_to_all x2, starting transfers between devices, exchange(): lax.all_to_all(wide, 'expert', split_axis=0, concat_axis=0, tiled=True)  15.7 us
    pallas_call x1, Pallas kernels, on_device(): pl.pallas_call(delta_body, grid=(GROUPS,), in_specs=[smem(), block, block...  9.96 us
    pallas_call x1, Pallas kernels, on_device(): pl.pallas_call(gradient_body, grid_spec=grid_spec(steps, [table, rows_spe...  8.98 us
    pallas_call x1, Pallas kernels, on_device(): pl.pallas_call(assemble_body, grid_spec=grid_spec(steps, [*laid, wide, wi...  5.53 us
    ppermute x1, starting transfers between devices, on_device(): g_near = lax.ppermute(g_away, 'core', swap)  5.41 us
  transfers between devices with their start and end apart: 19, of which 13 were waited for; matrix products, arithmetic and copies ran while one was open for 0% of the time, Pallas kernels for 2%

commit v1 on v0

--- a/solution.py
+++ b/solution.py
@@ -30,6 +30,8 @@
 GROUP = 4 * UNIT
 GROUPS = FF // GROUP
 PER_STEP = 4
+FLAG = 1
+DELTA_GROUPS = 2
 
 
 def iota(shape, dim):
@@ -165,29 +167,33 @@
 
 def delta_body(core, mean, rho, noise, own_ref, oth_ref):
     c = core[0]
-    delta = jnp.log(1.0 + jnp.exp(rho[0].astype(F32))) * noise[0].astype(F32)
     lane = iota((FEAT, WIDE), 1)
-    for which, x in ((0, mean[0].astype(F32)), (1, delta)):
-        for j in range(4):
-            start = UNIT * j
-            base = start // 128 * 128
-            off = start - base
-            width = min(GROUP - base, 384)
-            window = x[:, base : base + width]
-            if off:
-                window = pltpu.roll(window, width - off, 1)
-            chunk = jnp.where(lane < UNIT, window[:, :WIDE], 0.0).astype(BF16)
-
-            @pl.when(c == j % 2)
-            def _():
-                own_ref[which, j // 2] = chunk
-
-            @pl.when(c != j % 2)
-            def _():
-                oth_ref[which, j // 2] = chunk
-
-
-def forward_part(k, lin, rows, signed, words, weights, y_ref):
+    for g in range(DELTA_GROUPS):
+        lanes = slice(GROUP * g, GROUP * (g + 1))
+        u = jnp.exp(rho[0, :, lanes].astype(F32))
+        delta = jnp.log(1.0 + u) * noise[0, :, lanes].astype(F32)
+        for which, x in ((0, mean[0, :, lanes].astype(F32)), (1, delta)):
+            for j in range(4):
+                start = UNIT * j
+                base = start // 128 * 128
+                off = start - base
+                width = min(GROUP - base, 384)
+                window = x[:, base : base + width]
+                if off:
+                    window = pltpu.roll(window, width - off, 1)
+                chunk = jnp.where(lane < UNIT, window[:, :WIDE], 0.0).astype(BF16)
+                at = 2 * g + j // 2
+
+                @pl.when(c == j % 2)
+                def _():
+                    own_ref[which, at] = chunk
+
+                @pl.when(c != j % 2)
+                def _():
+                    oth_ref[which, at] = chunk
+
+
+def forward_part(k, lin, rows, signed, words, weights, halves):
     for l in range(4):
         mean, delta = (
             jnp.concatenate([weights[l][w, 0], weights[4 + l][w, 0]], axis=0) for w in range(2)
@@ -197,12 +203,12 @@
         base = WORDS * chunk_at(lin, k, l)
         y1 = m[:, :128] + flip(sign_bits(words, base), p[:, :128])
         y2 = m[:, 128:] + flip(sign_bits(words, base + 4), p[:, 128:])
-        y_ref[l, :SLOTS, :] = y1.astype(BF16)
-        y_ref[l, SLOTS:, :] = fold(y2).astype(BF16)
+        halves[l // 2][l % 2, :SLOTS, :] = y1.astype(BF16)
+        halves[l // 2][l % 2, SLOTS:, :] = fold(y2).astype(BF16)
 
 
 def forward_first(k, lin, got, *refs):
-    weights, (y_ref, words_ref, signed_ref) = refs[:8], refs[8:]
+    weights, halves, (words_ref, signed_ref) = refs[:8], refs[8:10], refs[10:]
     words = jnp.zeros((SLOTS, 128), I32)
     for j in range(4):
         at = 2 * WIDE + 128 * j
@@ -213,17 +219,22 @@
         bits = sign_bits(words, HALF_WORDS + 4 * side)
         a = got[:, FEAT * side : FEAT * (side + 1)].astype(F32)
         signed_ref[:, FEAT * side : FEAT * (side + 1)] = flip(bits, a).astype(BF16)
-    forward_part(k, lin[0], got[:, :WIDE], signed_ref[...], words_ref[...], weights, y_ref)
+    forward_part(k, lin[0], got[:, :WIDE], signed_ref[...], words_ref[...], weights, halves)
 
 
 def forward_next(k, lin, rows, signed, words, *refs):
-    forward_part(k, lin[0], rows[...], signed[...], words[...], refs[:8], refs[8])
-
-
-def halfway_body(p0, r1, r2, r3, q0, q1, q2, q3):
+    forward_part(k, lin[0], rows[...], signed[...], words[...], refs[:8], refs[8:10])
+
+
+def join_body(a, b, out_ref):
+    out_ref[...] = (a[...].astype(F32) + b[...].astype(F32)).astype(BF16)
+
+
+def halfway_body(low, low1, low3, high, high1, high3, q0, q1, q2, q3):
     for l, q in enumerate((q0, q1, q2, q3)):
-        total = p0[l].astype(F32) + r1[l].astype(F32)
-        total = total + (r2[l].astype(F32) + r3[l].astype(F32))
+        a, b, c = ((low, low1, low3), (high, high1, high3))[l // 2]
+        i = l % 2
+        total = a[i].astype(F32) + b[i].astype(F32) + c[i].astype(F32)
         q[...] = total.astype(q.dtype)
 
 
@@ -240,9 +251,9 @@
     dy_ref[SLOTS:, :] = fold(ds[1]).astype(BF16)
 
 
-def stack_body(a, b, c, d, out_ref):
+def stack_body(a, b, c, d, _, low_ref, high_ref):
     for i, x in enumerate((a, b, c, d)):
-        out_ref[i] = x[...]
+        (low_ref, high_ref)[i // 2][i % 2] = x[...]
 
 
 def gradient_chunk(words, dy, k):
@@ -260,52 +271,63 @@
     return plain, signed
 
 
-def gradient_body(lin, words, rows, v0, v1, v2, v3, *refs):
-    own, near = refs[:4], refs[4:8]
-    mine_ref, theirs_ref, g_ref, g_away_ref, rows_t, signed_t, sum_m, sum_d = refs[8:]
-    step = pl.program_id(0)
-
-    @pl.when(step == 0)
-    def _():
-        for side in range(2):
-            lanes = slice(FEAT * side, FEAT * (side + 1))
-            a = rows[:, lanes].astype(F32)
-            bits = sign_bits(words[...], HALF_WORDS + 4 * side)
-            rows_t[lanes, :] = a.T.astype(BF16)
-            signed_t[lanes, :] = flip(bits, a).T.astype(BF16)
-        sum_m[...] = jnp.zeros_like(sum_m)
-        sum_d[...] = jnp.zeros_like(sum_d)
-
+def gradient_part(k, lin, words, rows_t, signed_t, dys, weights, sums, mine_ref, theirs_ref):
     plains = []
     signeds = []
-    for i in range(PER_STEP):
-        dy = jnp.where(
-            step < 2,
-            jnp.where(step == 0, v0[i], v1[i]),
-            jnp.where(step == 2, v2[i], v3[i]),
-        )
-        plain, signed = gradient_chunk(words[...], dy, chunk_at(lin[0], -step, -i))
+    for l in range(4):
+        dy = dys[l // 2][l % 2]
+        plain, signed = gradient_chunk(words, dy, chunk_at(lin, -k, -l))
         plains.append(plain)
         signeds.append(signed)
-        for which, g in ((0, dot(rows_t[...], plain)), (1, dot(signed_t[...], signed))):
-            mine_ref[which, i] = g[:FEAT, :].astype(BF16)
-            theirs_ref[which, i] = g[FEAT:, :].astype(BF16)
-    for which, parts, total in ((0, plains, sum_m), (1, signeds, sum_d)):
-        weights = jnp.concatenate(
-            [
-                jnp.concatenate([w[which, 0] for w in side], axis=1)
-                for side in (own, near)
-            ],
-            axis=0,
+        for which, g in ((0, dot(rows_t, plain)), (1, dot(signed_t, signed))):
+            mine_ref[which, l] = g[:FEAT, :].astype(BF16)
+            theirs_ref[which, l] = g[FEAT:, :].astype(BF16)
+    out = []
+    for which, parts in ((0, plains), (1, signeds)):
+        side = [
+            jnp.concatenate([w[which, 0] for w in weights[at : at + 4]], axis=1) for at in (0, 4)
+        ]
+        total = dot(
+            jnp.concatenate(parts, axis=1), jnp.concatenate(side, axis=0), ((1,), (1,))
         )
-        total[...] += dot(jnp.concatenate(parts, axis=1), weights, ((1,), (1,)))
-
-    @pl.when(step == pl.num_programs(0) - 1)
-    def _():
-        for side, ref in ((0, g_ref), (1, g_away_ref)):
-            lanes = slice(FEAT * side, FEAT * (side + 1))
-            bits = sign_bits(words[...], HALF_WORDS + 4 * side)
-            ref[...] = sum_m[:, lanes] + flip(bits, sum_d[:, lanes])
+        out.append(total if sums is None else total + sums[which][...])
+    return out
+
+
+def gradient_first(lin, words, rows, low, high, *refs):
+    dys = (low, high)
+    weights, (mine, theirs, rows_t, signed_t, sum_m, sum_d) = refs[:8], refs[8:]
+    for side in range(2):
+        lanes = slice(FEAT * side, FEAT * (side + 1))
+        a = rows[:, lanes].astype(F32)
+        bits = sign_bits(words[...], HALF_WORDS + 4 * side)
+        rows_t[lanes, :] = a.T.astype(BF16)
+        signed_t[lanes, :] = flip(bits, a).T.astype(BF16)
+    sum_m[...], sum_d[...] = gradient_part(
+        0, lin[0], words[...], rows_t[...], signed_t[...], dys, weights, None, mine, theirs
+    )
+
+
+def gradient_next(k, lin, words, rows_t, signed_t, in_m, in_d, low, high, *refs):
+    dys = (low, high)
+    weights, (_, _, mine, theirs, sum_m, sum_d) = refs[:8], refs[8:]
+    sum_m[...], sum_d[...] = gradient_part(
+        k, lin[0], words[...], rows_t[...], signed_t[...], dys, weights, (in_m, in_d),
+        mine, theirs,
+    )
+
+
+def gradient_last(k, lin, words, rows_t, signed_t, in_m, in_d, low, high, *refs):
+    dys = (low, high)
+    weights, (_, _, mine, theirs, g_ref, g_away_ref) = refs[:8], refs[8:]
+    total_m, total_d = gradient_part(
+        k, lin[0], words[...], rows_t[...], signed_t[...], dys, weights, (in_m, in_d),
+        mine, theirs,
+    )
+    for side, ref in ((0, g_ref), (1, g_away_ref)):
+        lanes = slice(FEAT * side, FEAT * (side + 1))
+        bits = sign_bits(words[...], HALF_WORDS + 4 * side)
+        ref[...] = total_m[:, lanes] + flip(bits, total_d[:, lanes])
 
 
 def slots_body(g, g_near, hidden, send_ref):
@@ -393,11 +415,11 @@
     got = exchange(send)
 
     late, _ = lax.optimization_barrier((core, send))
-    block = pl.BlockSpec((1, FEAT, GROUP), lambda g: (0, 0, g))
-    pair = pl.BlockSpec((2, 2, FEAT, WIDE), lambda g: (0, g, 0, 0))
+    block = pl.BlockSpec((1, FEAT, DELTA_GROUPS * GROUP), lambda g: (0, 0, g))
+    pair = pl.BlockSpec((2, 2 * DELTA_GROUPS, FEAT, WIDE), lambda g: (0, g, 0, 0))
     own, away = pl.pallas_call(
         delta_body,
-        grid=(GROUPS,),
+        grid=(GROUPS // DELTA_GROUPS,),
         in_specs=[smem(), block, block, block],
         out_specs=(pair, pair),
         out_shape=(pltpu.HBM((2, CHIPS, FEAT, WIDE), BF16),) * 2,
@@ -410,8 +432,8 @@
     steps = CHIPS // PER_STEP
     table = whole(SLOTS, 128)
     rows_spec = pl.BlockSpec((SLOTS, WIDE), lambda *_: (0, 0))
-    quad = struct((4, PACK, 128), BF16)
-    quad_spec = whole(4, PACK, 128)
+    half = struct((2, PACK, 128), BF16)
+    half_spec = whole(2, PACK, 128)
     lone_spec = whole(PACK, 128)
 
     def picked(index):
@@ -425,42 +447,67 @@
             scratch_shapes=scratch,
         )
 
-    sent = [None] * 4
+    (own_far,) = far_memory(own)
+    sent = [[] for _ in range(4)]
     words = signed = None
-    for k in (1, 3, 2, 0):
+    for k in (2, 1, 3, 0):
         chunks = [
             picked(lambda lin, i, k=k, l=l: chunk_at(lin, k, l)) for l in range(4)
         ] * 2
         if words is None:
-            sent[k], words, signed = pl.pallas_call(
+            *sent[k], words, signed = pl.pallas_call(
                 functools.partial(forward_first, k),
                 grid_spec=grid_spec(
-                    1, [whole(SLOTS, 4 * WIDE), *chunks], (quad_spec, table, rows_spec)
+                    1, [whole(SLOTS, 4 * WIDE), *chunks], (half_spec, half_spec, table, rows_spec)
                 ),
-                out_shape=(quad, struct((SLOTS, 128), I32), struct((SLOTS, WIDE), BF16)),
+                out_shape=(
+                    half, half, struct((SLOTS, 128), I32), struct((SLOTS, WIDE), BF16)
+                ),
                 compiler_params=params("arbitrary"),
                 cost_estimate=cost(600_000_000, 2 << 20),
-            )(lin, got, *[own] * 4, *[near] * 4)
+            )(lin, got, *[own_far] * 4, *[near] * 4)
         else:
             sent[k] = pl.pallas_call(
                 functools.partial(forward_next, k),
-                grid_spec=grid_spec(1, [rows_spec, rows_spec, table, *chunks], quad_spec),
-                out_shape=quad,
+                grid_spec=grid_spec(
+                    1, [rows_spec, rows_spec, table, *chunks], (half_spec, half_spec)
+                ),
+                out_shape=(half, half),
                 compiler_params=params("arbitrary"),
                 cost_estimate=cost(600_000_000, 2 << 20),
             )(lin, got, signed, words, *[own] * 4, *[near] * 4)
-    parts = [sent[0]] + [hop(sent[k], k, True) for k in (1, 2, 3)]
+
+    def move(x, steps):
+        return hop(x, steps, True)
+
+    def joined(x, y):
+        return pl.pallas_call(
+            join_body,
+            grid=(1,),
+            in_specs=[half_spec, half_spec],
+            out_specs=half_spec,
+            out_shape=half,
+            compiler_params=params("arbitrary"),
+            cost_estimate=cost(50_000_000, 1 << 20),
+        )(x, y)
+
+    from_below = move(sent[2][0], 1)
+    from_above = move(sent[2][1], 3)
+    high1 = move(sent[1][1], 1)
+    low3 = move(sent[3][0], 3)
+    low1 = move(joined(sent[1][0], from_below), 1)
+    high3 = move(joined(sent[3][1], from_above), 3)
     lone = struct((PACK, 128), BF16)
     kept, *passed = pl.pallas_call(
         halfway_body,
         grid=(1,),
-        in_specs=[quad_spec] * 4,
+        in_specs=[half_spec] * 6,
         out_specs=(lone_spec,) * 4,
         out_shape=(struct((PACK, 128), F32), lone, lone, lone),
         compiler_params=params("arbitrary"),
         cost_estimate=cost(200_000_000, 3 << 20),
         name="halfway",
-    )(*parts)
+    )(sent[0][0], low1, low3, sent[0][1], high1, high3)
     passed = [hop(passed[l - 1], l, False) for l in (1, 2, 3)]
     hidden, dy = pl.pallas_call(
         middle_body,
@@ -472,35 +519,68 @@
         cost_estimate=cost(200_000_000, 1 << 20),
         name="middle",
     )(kept, *passed, got)
-    stack = pl.pallas_call(
+    beside = [hop(dy, l, False) for l in (1, 2, 3)]
+    partner = lax.ppermute(beside[FLAG], "core", swap)
+    low, high = pl.pallas_call(
         stack_body,
         grid=(1,),
-        in_specs=[lone_spec] * 4,
-        out_specs=quad_spec,
-        out_shape=quad,
+        in_specs=[lone_spec] * 4 + [pl.BlockSpec(memory_space=pl.ANY)],
+        out_specs=(half_spec, half_spec),
+        out_shape=(half, half),
         compiler_params=params("arbitrary"),
         cost_estimate=cost(100_000_000, 1 << 20),
         name="stack",
-    )(dy, *[hop(dy, l, False) for l in (1, 2, 3)])
-    dys = [stack] + [hop(stack, k, True) for k in (1, 2, 3)]
+    )(dy, *beside, partner)
+    low1 = move(low, 1)
+    high3 = move(high, 3)
+    high1 = move(high, 1)
+    low3 = move(low, 3)
+    low2 = move(low1, 1)
+    high2 = move(high3, 3)
+    dys = [(low, high), (low1, high1), (low2, high2), (low3, high3)]
 
     sums = whole(SLOTS, FEAT)
+    wide_sums = whole(SLOTS, WIDE)
+    turned = whole(WIDE, SLOTS)
     side = pltpu.HBM((2, CHIPS, FEAT, WIDE), BF16)
-    weights = pl.BlockSpec((2, PER_STEP, FEAT, WIDE), lambda k, lin: (0, k, 0, 0))
-    chunks = [picked(lambda lin, i, l=l: chunk_at(lin, -i, -l)) for l in range(4)] * 2
-    mine, theirs, g, g_away = pl.pallas_call(
-        gradient_body,
-        grid_spec=grid_spec(
-            steps,
-            [table, rows_spec] + [quad_spec] * 4 + chunks,
-            (weights, weights, sums, sums),
-            [pltpu.VMEM((WIDE, SLOTS), BF16)] * 2 + [pltpu.VMEM((SLOTS, WIDE), F32)] * 2,
-        ),
-        out_shape=(side, side, struct((SLOTS, FEAT), F32), struct((SLOTS, FEAT), F32)),
-        compiler_params=params("arbitrary"),
-        cost_estimate=cost(5_000_000_000, 12 << 20),
-        name="backward",
-    )(lin, words, got, *dys, *[own] * 4, *[near] * 4)
+    in_place = pl.BlockSpec(memory_space=pltpu.HBM)
+    turned_shape = struct((WIDE, SLOTS), BF16)
+    total_shape = struct((SLOTS, WIDE), F32)
+    slot_shape = struct((SLOTS, FEAT), F32)
+    for k in (0, 1, 3, 2):
+        chunks = [
+            picked(lambda lin, i, k=k, l=l: chunk_at(lin, -k, -l)) for l in range(4)
+        ] * 2
+        block = pl.BlockSpec((2, 4, FEAT, WIDE), lambda i, lin, k=k: (0, k, 0, 0))
+        last = k == 2
+        if k == 0:
+            body = gradient_first
+            ins = [table, rows_spec, half_spec, half_spec, *chunks]
+            outs = (turned, turned, wide_sums, wide_sums)
+            shapes = (turned_shape, turned_shape, total_shape, total_shape)
+            operands = (words, got, *dys[k])
+            carried = ()
+        else:
+            body = functools.partial(gradient_last if last else gradient_next, k)
+            ins = [table, turned, turned, wide_sums, wide_sums, half_spec, half_spec, *chunks]
+            ins += [in_place, in_place]
+            outs = (sums, sums) if last else (wide_sums, wide_sums)
+            shapes = (slot_shape,) * 2 if last else (total_shape,) * 2
+            operands = (words, rows_t, signed_t, *totals, *dys[k])
+            carried = (mine, theirs)
+        got_back = pl.pallas_call(
+            body,
+            grid_spec=grid_spec(1, ins, (block, block, *outs)),
+            out_shape=(side, side, *shapes),
+            input_output_aliases={len(ins) - 1: 0, len(ins): 1} if carried else {},
+            compiler_params=params("arbitrary"),
+            cost_estimate=cost(1_300_000_000, 3 << 20),
+        )(lin, *operands, *[own] * 4, *[near] * 4, *carried)
+        mine, theirs, *rest = got_back
+        if k == 0:
+            rows_t, signed_t, *rest = rest
+        totals = rest
+    g, g_away = totals
     g_near = lax.ppermute(g_away, "core", swap)
     theirs, _ = lax.optimization_barrier((theirs, g_near))
     theirs = lax.ppermute(theirs, "core", swap)
@@ -529,7 +609,7 @@
         compiler_params=params("arbitrary"),
         cost_estimate=cost(3_000_000_000, 12 << 20, FEAT * FF),
         name="assemble",
-    )(late, *[mine] * 4, *[theirs] * 4, rho_weight, noise_weight)
+    )(late, *far_memory(*[mine] * 4), *[theirs] * 4, rho_weight, noise_weight)
 
     hidden_out, grad_tokens = pl.pallas_call(
         combine_body,

time: 149 us -> 134 us (0.90)
  waiting for transfers between devices: 70.4 us -> 50 us
  starting transfers between devices: 41.5 us -> 47.8 us
  local copies, waits for them, and re-layouts: 3.19 us -> 0.01 us
  Pallas kernels: 32.7 us -> 34.7 us
    ppermute x12 -> x18, waiting for transfers between devices: 35.5 us -> 14 us  [hop(): return lax.ppermute(array, ('x', 'y', 'core'), pairs)]
    ppermute x12 -> x18, starting transfers between devices: 16.5 us -> 24.6 us  [hop(): return lax.ppermute(array, ('x', 'y', 'core'), pairs)]
    ppermute x0 -> x1, starting transfers between devices: none -> 7.53 us  [on_device(): partner = lax.ppermute(beside[FLAG], 'core', swap)]
    all_to_all x2, starting transfers between devices: 15.7 us -> 9.89 us  [exchange(): lax.all_to_all(wide, 'expert', split_axis=0, concat_axis=0, tiled=True)]
    ppermute x1, starting transfers between devices: 5.41 us -> 1.89 us  [on_device(): g_near = lax.ppermute(g_away, 'core', swap)]
    unnamed x6 -> x2, local copies, waits for them, and re-layouts: 3.19 us -> 0.01 us
    pallas_call x4 -> x9, Pallas kernels: 19.3 us -> 19.6 us  [the longest x4 10.5 us: on_device(): pl.pallas_call(body, grid_spec=grid_spec(1, ins, (block, block, *outs)),...]
  transfers between devices with their start and end apart: 19 -> 26, of which waited for: 13 -> 13; matrix products, arithmetic and copies ran while one was open for 0% -> 0% of each run, Pallas kernels for 2% -> 9%
where the time goes in v1:
time: 134 us; the launch traced here: 133 us
  waiting for transfers between devices  50 us (37%)
  starting transfers between devices  47.8 us (36%)
  Pallas kernels  34.7 us (26%)
    all_to_all x2, waiting for transfers between devices, exchange(): lax.all_to_all(wide, 'expert', split_axis=0, concat_axis=0, tiled=True)  32.7 us
    ppermute x18, starting transfers between devices, hop(): return lax.ppermute(array, ('x', 'y', 'core'), pairs)  24.6 us
    ppermute x18, waiting for transfers between devices, hop(): return lax.ppermute(array, ('x', 'y', 'core'), pairs)  14 us
    pallas_call x4, Pallas kernels, on_device(): pl.pallas_call(body, grid_spec=grid_spec(1, ins, (block, block, *outs)),...  10.5 us
    all_to_all x2, starting transfers between devices, exchange(): lax.all_to_all(wide, 'expert', split_axis=0, concat_axis=0, tiled=True)  9.89 us
    pallas_call x1, Pallas kernels, on_device(): pl.pallas_call(delta_body, grid=(GROUPS // DELTA_GROUPS,), in_specs=[smem...  8.65 us
    ppermute x1, starting transfers between devices, on_device(): partner = lax.ppermute(beside[FLAG], 'core', swap)  7.53 us
    pallas_call x1, Pallas kernels, on_device(): pl.pallas_call(assemble_body, grid_spec=grid_spec(steps, [*laid, wide, wi...  5.99 us
  transfers between devices with their start and end apart: 26, of which 13 were waited for; matrix products, arithmetic and copies ran while one was open for 0% of the time, Pallas kernels for 9%

profile of v1, /device:TPU:1, one launch (start us, length us, event | category | flops | bytes accessed | tf_op | source)
XLA Modules:
  0.0 133.3 jit_solution(992378302048301575)
XLA Ops:
  0.6 3.3 %collective-permute-start = (bf16[128,128]{1,0:T(8,128)(2,1)}, bf16[128,128]{1,0:T(8,128)(2,1)S(1)}, u32[]{:S(2)}, u32[]{:S(2)}) collective-permute-start(bf16[128,128]{1,0:T(8,128)(2,1)} %tok.1), channel_id=1, source_target_pairs={{0,8},{8,0},{1,9},{9,1},{2,10},{10,2},{3,11},{11,3},{4,12},{12,4},... | collective-permute-start | bytes 98312 | tf_op jit(solution)/shard_map/ppermute | solution.py:394
  5.3 2.6 %dispatch.1 = bf16[320,1024]{1,0:T(8,128)(2,1)} custom-call(s32[1]{0:T(128)} %bitcast.3.core, s32[2,128]{1,0:T(2,128)} %bitcast.23, f32[2,128]{1,0:T(2,128)} %bitcast.25, bf16[128,128]{1,0:T(8,128)(2,1)} %tok.1, bf16[128,128]{1,0:T(8,128)(2,1)S(1)} %collective-permute-done.tok_o, s32[4,128]{1,0:T(4,128)} %bitcast.22, ...), custom_call_target="tpu_custom_call" | custom-call | flops 400000000 | bytes 1048576 | tf_op jit(solution)/shard_map/dispatch/pallas_call | solution.py:399
  7.9 8.6 %delta.1 = (bf16[2,16,128,256]{3,2,1,0:T(8,128)(2,1)}, bf16[2,16,128,256]{3,2,1,0:T(8,128)(2,1)}) custom-call(s32[1]{0:T(128)} %bitcast.3.core, bf16[1,128,7168]{2,1,0:T(8,128)(2,1)} %mean.1, bf16[1,128,7168]{2,1,0:T(8,128)(2,1)} %refs_8_.1, bf16[1,128,7168]{2,1,0:T(8,128)(2,1)} %refs_9_.1), custom_call_target="tpu_custom_call" | custom-call | flops 2000000000 | bytes 10485760 | tf_op jit(solution)/shard_map/delta/pallas_call | solution.py:420
  16.7 6.5 %all-to-all-start = ((bf16[8,40,1024]{2,1,0:T(8,128)(2,1)}), bf16[8,40,1024]{2,1,0:T(8,128)(2,1)S(1)}, u32[]{:S(2)}, u32[]{:S(2)}) async-start(bf16[8,40,1024]{2,1,0:T(8,128)(2,1)} %bitcast.7), calls=%async_computation | async-start | bytes 1310720 | tf_op jit(solution)/shard_map/all_to_all | solution.py:412
  23.2 20.8 %all-to-all-done = bf16[8,40,1024]{2,1,0:T(8,128)(2,1)S(1)} async-done(((bf16[8,40,1024]{2,1,0:T(8,128)(2,1)}), bf16[8,40,1024]{2,1,0:T(8,128)(2,1)S(1)}, u32[]{:S(2)}, u32[]{:S(2)}) %all-to-all-start) | async-done | bytes 655392 | tf_op jit(solution)/shard_map/all_to_all | solution.py:412
  43.9 2.0 %shard_map.120 = (bf16[2,560,128]{2,1,0:T(8,128)(2,1)S(1)}, bf16[2,560,128]{2,1,0:T(8,128)(2,1)S(1)}, s32[320,128]{1,0:T(8,128)S(1)}, bf16[320,256]{1,0:T(8,128)(2,1)S(1)}) custom-call(s32[1]{0:T(128)} %bitcast.2.lin, bf16[320,1024]{1,0:T(8,128)(2,1)S(1)} %bitcast.12, bf16[2,16,128,256]{3,2,1,0:T(8,128)(2,1)} %get-tuple-element.50.refs_0_.refs_1_.refs_2_.refs_3_, ...), custom_call_target="tpu_custom_call" | custom-call | flops 600000000 | bytes 2097152 | tf_op jit(solution)/shard_map/pallas_call | solution.py:458
  46.0 2.6 %collective-permute-start.7 = (bf16[2,560,128]{2,1,0:T(8,128)(2,1)S(1)}, bf16[2,560,128]{2,1,0:T(8,128)(2,1)S(1)}, u32[]{:S(2)}, u32[]{:S(2)}) collective-permute-start(bf16[2,560,128]{2,1,0:T(8,128)(2,1)S(1)} %get-tuple-element.61), channel_id=1, source_target_pairs={{0,48},{8,200},{16,0},{24,216},{32,16},{40,232},{48,32},{56,248},{... | collective-permute-start | bytes 860168 | tf_op jit(solution)/shard_map/ppermute | solution.py:132
  49.1 2.8 %collective-permute-start.5 = (bf16[2,560,128]{2,1,0:T(8,128)(2,1)S(1)}, bf16[2,560,128]{2,1,0:T(8,128)(2,1)S(1)}, u32[]{:S(2)}, u32[]{:S(2)}) collective-permute-start(bf16[2,560,128]{2,1,0:T(8,128)(2,1)S(1)} %get-tuple-element.57), channel_id=1, source_target_pairs={{0,48},{8,200},{16,0},{24,216},{32,16},{40,232},{48,32},{56,248},{... | collective-permute-start | bytes 860168 | tf_op jit(solution)/shard_map/ppermute | solution.py:132
  52.7 2.7 %collective-permute-start.8 = (bf16[2,560,128]{2,1,0:T(8,128)(2,1)S(1)}, bf16[2,560,128]{2,1,0:T(8,128)(2,1)S(1)}, u32[]{:S(2)}, u32[]{:S(2)}) collective-permute-start(bf16[2,560,128]{2,1,0:T(8,128)(2,1)S(1)} %shard_map.125), channel_id=1, source_target_pairs={{0,48},{8,200},{16,0},{24,216},{32,16},{40,232},{48,32},{56,248},{... | collective-permute-start | bytes 860168 | tf_op jit(solution)/shard_map/ppermute | solution.py:132
  56.3 3.3 %collective-permute-done.6.high1 = bf16[2,560,128]{2,1,0:T(8,128)(2,1)S(1)} collective-permute-done((bf16[2,560,128]{2,1,0:T(8,128)(2,1)S(1)}, bf16[2,560,128]{2,1,0:T(8,128)(2,1)S(1)}, u32[]{:S(2)}, u32[]{:S(2)}) %collective-permute-start.6) | collective-permute-done | bytes 286752 | tf_op jit(solution)/shard_map/ppermute | solution.py:132
  59.6 3.1 %collective-permute-done.4.low1 = bf16[2,560,128]{2,1,0:T(8,128)(2,1)S(1)} collective-permute-done((bf16[2,560,128]{2,1,0:T(8,128)(2,1)S(1)}, bf16[2,560,128]{2,1,0:T(8,128)(2,1)S(1)}, u32[]{:S(2)}, u32[]{:S(2)}) %collective-permute-start.4) | collective-permute-done | bytes 286752 | tf_op jit(solution)/shard_map/ppermute | solution.py:132
  62.9 2.7 %collective-permute-start.10 = (bf16[560,128]{1,0:T(8,128)(2,1)S(1)}, bf16[560,128]{1,0:T(8,128)(2,1)S(1)}, u32[]{:S(2)}, u32[]{:S(2)}) collective-permute-start(bf16[560,128]{1,0:T(8,128)(2,1)S(1)} %get-tuple-element.64), channel_id=1, source_target_pairs={{0,128},{8,40},{16,144},{24,56},{32,160},{40,8},{48,176},{56,24},{... | collective-permute-start | bytes 430088 | tf_op jit(solution)/shard_map/ppermute | solution.py:132
  67.1 1.4 %collective-permute-done.10.t2 = bf16[560,128]{1,0:T(8,128)(2,1)S(1)} collective-permute-done((bf16[560,128]{1,0:T(8,128)(2,1)S(1)}, bf16[560,128]{1,0:T(8,128)(2,1)S(1)}, u32[]{:S(2)}, u32[]{:S(2)}) %collective-permute-start.10) | collective-permute-done | bytes 143392 | tf_op jit(solution)/shard_map/ppermute | solution.py:132
  68.4 1.7 %collective-permute-done.11.t3 = bf16[560,128]{1,0:T(8,128)(2,1)S(1)} collective-permute-done((bf16[560,128]{1,0:T(8,128)(2,1)S(1)}, bf16[560,128]{1,0:T(8,128)(2,1)S(1)}, u32[]{:S(2)}, u32[]{:S(2)}) %collective-permute-start.11) | collective-permute-done | bytes 143392 | tf_op jit(solution)/shard_map/ppermute | solution.py:132
  70.2 1.4 %collective-permute-done.9.t1 = bf16[560,128]{1,0:T(8,128)(2,1)S(1)} collective-permute-done((bf16[560,128]{1,0:T(8,128)(2,1)S(1)}, bf16[560,128]{1,0:T(8,128)(2,1)S(1)}, u32[]{:S(2)}, u32[]{:S(2)}) %collective-permute-start.9) | collective-permute-done | bytes 143392 | tf_op jit(solution)/shard_map/ppermute | solution.py:132
  71.8 1.4 %collective-permute-start.13 = (bf16[560,128]{1,0:T(8,128)(2,1)S(1)}, bf16[560,128]{1,0:T(8,128)(2,1)S(1)}, u32[]{:S(2)}, u32[]{:S(2)}) collective-permute-start(bf16[560,128]{1,0:T(8,128)(2,1)S(1)} %get-tuple-element.66.a), channel_id=1, source_target_pairs={{0,128},{8,40},{16,144},{24,56},{32,160},{40,8},{48,176},{56,24},{... | collective-permute-start | bytes 430088 | tf_op jit(solution)/shard_map/ppermute | solution.py:132
  73.8 2.1 %collective-permute-start.14 = (bf16[560,128]{1,0:T(8,128)(2,1)S(1)}, bf16[560,128]{1,0:T(8,128)(2,1)S(1)}, u32[]{:S(2)}, u32[]{:S(2)}) collective-permute-start(bf16[560,128]{1,0:T(8,128)(2,1)S(1)} %get-tuple-element.66.a), channel_id=1, source_target_pairs={{0,192},{8,56},{16,208},{24,8},{32,224},{40,24},{48,240},{56,40},{... | collective-permute-start | bytes 430088 | tf_op jit(solution)/shard_map/ppermute | solution.py:132
  75.9 1.5 %collective-permute-done.13.c = bf16[560,128]{1,0:T(8,128)(2,1)S(1)} collective-permute-done((bf16[560,128]{1,0:T(8,128)(2,1)S(1)}, bf16[560,128]{1,0:T(8,128)(2,1)S(1)}, u32[]{:S(2)}, u32[]{:S(2)}) %collective-permute-start.13) | collective-permute-done | bytes 143392 | tf_op jit(solution)/shard_map/ppermute | solution.py:132
  77.4 7.5 %collective-permute-start.15 = (bf16[560,128]{1,0:T(8,128)(2,1)S(1)}, bf16[560,128]{1,0:T(8,128)(2,1)S(1)}, u32[]{:S(2)}, u32[]{:S(2)}) collective-permute-start(bf16[560,128]{1,0:T(8,128)(2,1)S(1)} %collective-permute-done.13.c), channel_id=1, source_target_pairs={{0,8},{8,0},{1,9},{9,1},{2,10},{10,2},{3,11},{11,3},{4,12},{12,4},... | collective-permute-start | bytes 430088 | tf_op jit(solution)/shard_map/ppermute | solution.py:523
  86.0 2.7 %collective-permute-start.19 = (bf16[2,560,128]{2,1,0:T(8,128)(2,1)S(1)}, bf16[2,560,128]{2,1,0:T(8,128)(2,1)S(1)}, u32[]{:S(2)}, u32[]{:S(2)}) collective-permute-start(bf16[2,560,128]{2,1,0:T(8,128)(2,1)S(1)} %get-tuple-element.68.high), channel_id=1, source_target_pairs={{0,48},{8,200},{16,0},{24,216},{32,16},{40,232},{48,32},{56,248},{... | collective-permute-start | bytes 860168 | tf_op jit(solution)/shard_map/ppermute | solution.py:132
  88.7 2.7 %collective-permute-start.18 = (bf16[2,560,128]{2,1,0:T(8,128)(2,1)S(1)}, bf16[2,560,128]{2,1,0:T(8,128)(2,1)S(1)}, u32[]{:S(2)}, u32[]{:S(2)}) collective-permute-start(bf16[2,560,128]{2,1,0:T(8,128)(2,1)S(1)} %get-tuple-element.67.low), channel_id=1, source_target_pairs={{0,48},{8,200},{16,0},{24,216},{32,16},{40,232},{48,32},{56,248},{... | collective-permute-start | bytes 860168 | tf_op jit(solution)/shard_map/ppermute | solution.py:132
  91.4 1.6 %collective-permute-done.16.low = bf16[2,560,128]{2,1,0:T(8,128)(2,1)S(1)} collective-permute-done((bf16[2,560,128]{2,1,0:T(8,128)(2,1)S(1)}, bf16[2,560,128]{2,1,0:T(8,128)(2,1)S(1)}, u32[]{:S(2)}, u32[]{:S(2)}) %collective-permute-start.16) | collective-permute-done | bytes 286752 | tf_op jit(solution)/shard_map/ppermute | solution.py:132
  93.0 2.7 %collective-permute-start.21 = (bf16[2,560,128]{2,1,0:T(8,128)(2,1)S(1)}, bf16[2,560,128]{2,1,0:T(8,128)(2,1)S(1)}, u32[]{:S(2)}, u32[]{:S(2)}) collective-permute-start(bf16[2,560,128]{2,1,0:T(8,128)(2,1)S(1)} %collective-permute-done.19.high), channel_id=1, source_target_pairs={{0,48},{8,200},{16,0},{24,216},{32,16},{40,232},{48,32},{56,248},{... | collective-permute-start | bytes 860168 | tf_op jit(solution)/shard_map/ppermute | solution.py:132
  95.7 2.8 %shard_map.126 = (bf16[2,16,128,256]{3,2,1,0:T(8,128)(2,1)}, bf16[2,16,128,256]{3,2,1,0:T(8,128)(2,1)}, bf16[256,320]{1,0:T(8,128)(2,1)S(1)}, bf16[256,320]{1,0:...) custom-call(s32[1]{0:T(128)} %bitcast.2.lin, s32[320,128]{1,0:T(8,128)S(1)} %get-tuple-element.52.words, ...), custom_call_target="tpu_custom_call" | custom-call | flops 1300000000 | bytes 3145728 | tf_op jit(solution)/shard_map/pallas_call | solution.py:571
  98.5 2.5 %shard_map.127 = (bf16[2,16,128,256]{3,2,1,0:T(8,128)(2,1)}, bf16[2,16,128,256]{3,2,1,0:T(8,128)(2,1)}, f32[320,256]{1,0:T(8,128)S(1)}, f32[320,256]{1,0:T(8,128)S(1)}) custom-call(s32[1]{0:T(128)} %bitcast.2.lin, s32[320,128]{1,0:T(8,128)S(1)} %get-tuple-element.52.words, ...), custom_call_target="tpu_custom_call", output_to_operand_aliasing={{0}: (16, {}), {1}: (17, {})} | custom-call | flops 1300000000 | bytes 3145728 | tf_op jit(solution)/shard_map/pallas_call | solution.py:571
  101.1 2.6 %shard_map.128 = (bf16[2,16,128,256]{3,2,1,0:T(8,128)(2,1)}, bf16[2,16,128,256]{3,2,1,0:T(8,128)(2,1)}, f32[320,256]{1,0:T(8,128)S(1)}, f32[320,256]{1,0:T(8,128)S(1)}) custom-call(s32[1]{0:T(128)} %bitcast.2.lin, s32[320,128]{1,0:T(8,128)S(1)} %get-tuple-element.52.words, ...), custom_call_target="tpu_custom_call", output_to_operand_aliasing={{0}: (16, {}), {1}: (17, {})} | custom-call | flops 1300000000 | bytes 3145728 | tf_op jit(solution)/shard_map/pallas_call | solution.py:571
  103.7 2.6 %shard_map.129 = (bf16[2,16,128,256]{3,2,1,0:T(8,128)(2,1)}, bf16[2,16,128,256]{3,2,1,0:T(8,128)(2,1)}, f32[320,128]{1,0:T(8,128)S(1)}, f32[320,128]{1,0:T(8,128)S(1)}) custom-call(s32[1]{0:T(128)} %bitcast.2.lin, s32[320,128]{1,0:T(8,128)S(1)} %get-tuple-element.52.words, ...), custom_call_target="tpu_custom_call", output_to_operand_aliasing={{0}: (16, {}), {1}: (17, {})} | custom-call | flops 1300000000 | bytes 3145728 | tf_op jit(solution)/shard_map/pallas_call | solution.py:571
  106.2 1.9 %collective-permute-start.22 = (f32[320,128]{1,0:T(8,128)S(1)}, f32[320,128]{1,0:T(8,128)S(1)}, u32[]{:S(2)}, u32[]{:S(2)}) collective-permute-start(f32[320,128]{1,0:T(8,128)S(1)} %get-tuple-element.84), channel_id=1, source_target_pairs={{0,8},{8,0},{1,9},{9,1},{2,10},{10,2},{3,11},{11,3},{4,12},{12,4},... | collective-permute-start | bytes 491528 | tf_op jit(solution)/shard_map/ppermute | solution.py:584
  110.2 3.4 %all-to-all-start.1 = ((bf16[8,40,384]{2,1,0:T(8,128)(2,1)}), bf16[8,40,384]{2,1,0:T(8,128)(2,1)S(1)}, u32[]{:S(2)}, u32[]{:S(2)}) async-start(bf16[8,40,384]{2,1,0:T(8,128)(2,1)} %bitcast.9), calls=%async_computation.1 | async-start | bytes 491520 | tf_op jit(solution)/shard_map/all_to_all | solution.py:412
  113.6 11.9 %all-to-all-done.1 = bf16[8,40,384]{2,1,0:T(8,128)(2,1)S(1)} async-done(((bf16[8,40,384]{2,1,0:T(8,128)(2,1)}), bf16[8,40,384]{2,1,0:T(8,128)(2,1)S(1)}, u32[]{:S(2)}, u32[]{:S(2)}) %all-to-all-start.1) | async-done | bytes 245792 | tf_op jit(solution)/shard_map/all_to_all | solution.py:412
  125.6 1.7 %combine.1 = (bf16[224,128]{1,0:T(8,128)(2,1)}, bf16[128,128]{1,0:T(8,128)(2,1)}) custom-call(s32[2,128]{1,0:T(2,128)} %bitcast.24, f32[2,128]{1,0:T(2,128)} %bitcast.26, bf16[320,384]{1,0:T(8,128)(2,1)S(1)} %bitcast.18), custom_call_target="tpu_custom_call" | custom-call | flops 200000000 | bytes 524288 | tf_op jit(solution)/shard_map/combine/pallas_call | solution.py:614
  127.3 6.0 %assemble.1 = (bf16[1,128,7168]{2,1,0:T(8,128)(2,1)}, bf16[1,128,7168]{2,1,0:T(8,128)(2,1)}) custom-call(s32[1]{0:T(128)} %bitcast.2.lin, bf16[2,16,128,256]{3,2,1,0:T(8,128)(2,1)} %get-tuple-element.89.refs_0_.refs_1_.refs_2_.refs_3_, bf16[2,16,128,256]{3,2,1,0:T(8,128)(2,1)} %get-tuple-element.89.refs_0_.refs_1_.refs_2_.refs_3_, ...), custom_call_target="tpu_custom_call" | custom-call | flops 3000000000 | bytes 12582912 | tf_op jit(solution)/shard_map/assemble/pallas_call | solution.py:605
  (40 shorter events, 9.5 us)
Async XLA Ops:
  0.6 4.7 %collective-permute-start = (bf16[128,128]{1,0:T(8,128)(2,1)}, bf16[128,128]{1,0:T(8,128)(2,1)S(1)}, u32[]{:S(2)}, u32[]{:S(2)}) collective-permute-start(bf16[128,128]{1,0:T(8,128)(2,1)} %tok.1), channel_id=1, source_target_pairs={{0,8},{8,0},{1,9},{9,1},{2,10},{10,2},{3,11},{11,3},{4,12},{12,4},... | collective-permute-start | bytes 98312 | tf_op jit(solution)/shard_map/ppermute | solution.py:394
  3.9 1.4 %collective-permute-start.1 = (s32[4,128]{1,0:T(4,128)}, s32[4,128]{1,0:T(4,128)S(1)}, u32[]{:S(2)}, u32[]{:S(2)}) collective-permute-start(s32[4,128]{1,0:T(4,128)} %bitcast.21), channel_id=1, source_target_pairs={{0,8},{8,0},{1,9},{9,1},{2,10},{10,2},{3,11},{11,3},{4,12},{12,4},... | collective-permute-start | bytes 6152 | tf_op jit(solution)/shard_map/ppermute | solution.py:395
  16.5 27.4 %collective-permute-start.2 = (bf16[2,16,128,256]{3,2,1,0:T(8,128)(2,1)}, bf16[2,16,128,256]{3,2,1,0:T(8,128)(2,1)S(1)}, u32[]{:S(2)}, u32[]{:S(2)}) collective-permute-start(bf16[2,16,128,256]{3,2,1,0:T(8,128)(2,1)} %get-tuple-element.51), channel_id=1, source_target_pairs={{0,8},{8,0},{1,9},{9,1},{2,10},{10,2},{3,11},{11,3},{4,12},{12,4},... | collective-permute-start | bytes 6291464 | tf_op jit(solution)/shard_map/ppermute | solution.py:430
  16.7 27.2 %all-to-all-start = ((bf16[8,40,1024]{2,1,0:T(8,128)(2,1)}), bf16[8,40,1024]{2,1,0:T(8,128)(2,1)S(1)}, u32[]{:S(2)}, u32[]{:S(2)}) async-start(bf16[8,40,1024]{2,1,0:T(8,128)(2,1)} %bitcast.7), calls=%async_computation | async-start | bytes 1310720 | tf_op jit(solution)/shard_map/all_to_all | solution.py:412
  43.9 4.6 %copy-start = (bf16[2,16,128,256]{3,2,1,0:T(8,128)(2,1)S(1)}, bf16[2,16,128,256]{3,2,1,0:T(8,128)(2,1)}, u32[]{:S(2)}) copy-start(bf16[2,16,128,256]{3,2,1,0:T(8,128)(2,1)} %get-tuple-element.50.refs_0_.refs_1_.refs_2_.refs_3_) | copy-start | bytes 6291460
  46.0 6.7 %collective-permute-start.7 = (bf16[2,560,128]{2,1,0:T(8,128)(2,1)S(1)}, bf16[2,560,128]{2,1,0:T(8,128)(2,1)S(1)}, u32[]{:S(2)}, u32[]{:S(2)}) collective-permute-start(bf16[2,560,128]{2,1,0:T(8,128)(2,1)S(1)} %get-tuple-element.61), channel_id=1, source_target_pairs={{0,48},{8,200},{16,0},{24,216},{32,16},{40,232},{48,32},{56,248},{... | collective-permute-start | bytes 860168 | tf_op jit(solution)/shard_map/ppermute | solution.py:132
  48.5 7.0 %collective-permute-start.3 = (bf16[2,560,128]{2,1,0:T(8,128)(2,1)S(1)}, bf16[2,560,128]{2,1,0:T(8,128)(2,1)S(1)}, u32[]{:S(2)}, u32[]{:S(2)}) collective-permute-start(bf16[2,560,128]{2,1,0:T(8,128)(2,1)S(1)} %get-tuple-element.56), channel_id=1, source_target_pairs={{0,16},{8,72},{16,32},{24,88},{32,48},{40,104},{48,0},{56,120},{64... | collective-permute-start | bytes 860168 | tf_op jit(solution)/shard_map/ppermute | solution.py:132
  49.1 7.2 %collective-permute-start.5 = (bf16[2,560,128]{2,1,0:T(8,128)(2,1)S(1)}, bf16[2,560,128]{2,1,0:T(8,128)(2,1)S(1)}, u32[]{:S(2)}, u32[]{:S(2)}) collective-permute-start(bf16[2,560,128]{2,1,0:T(8,128)(2,1)S(1)} %get-tuple-element.57), channel_id=1, source_target_pairs={{0,48},{8,200},{16,0},{24,216},{32,16},{40,232},{48,32},{56,248},{... | collective-permute-start | bytes 860168 | tf_op jit(solution)/shard_map/ppermute | solution.py:132
  52.5 7.1 %collective-permute-start.6 = (bf16[2,560,128]{2,1,0:T(8,128)(2,1)S(1)}, bf16[2,560,128]{2,1,0:T(8,128)(2,1)S(1)}, u32[]{:S(2)}, u32[]{:S(2)}) collective-permute-start(bf16[2,560,128]{2,1,0:T(8,128)(2,1)S(1)} %get-tuple-element.59), channel_id=1, source_target_pairs={{0,16},{8,72},{16,32},{24,88},{32,48},{40,104},{48,0},{56,120},{64... | collective-permute-start | bytes 860168 | tf_op jit(solution)/shard_map/ppermute | solution.py:132
  52.7 6.9 %collective-permute-start.8 = (bf16[2,560,128]{2,1,0:T(8,128)(2,1)S(1)}, bf16[2,560,128]{2,1,0:T(8,128)(2,1)S(1)}, u32[]{:S(2)}, u32[]{:S(2)}) collective-permute-start(bf16[2,560,128]{2,1,0:T(8,128)(2,1)S(1)} %shard_map.125), channel_id=1, source_target_pairs={{0,48},{8,200},{16,0},{24,216},{32,16},{40,232},{48,32},{56,248},{... | collective-permute-start | bytes 860168 | tf_op jit(solution)/shard_map/ppermute | solution.py:132
  55.6 7.1 %collective-permute-start.4 = (bf16[2,560,128]{2,1,0:T(8,128)(2,1)S(1)}, bf16[2,560,128]{2,1,0:T(8,128)(2,1)S(1)}, u32[]{:S(2)}, u32[]{:S(2)}) collective-permute-start(bf16[2,560,128]{2,1,0:T(8,128)(2,1)S(1)} %shard_map.123), channel_id=1, source_target_pairs={{0,16},{8,72},{16,32},{24,88},{32,48},{40,104},{48,0},{56,120},{64... | collective-permute-start | bytes 860168 | tf_op jit(solution)/shard_map/ppermute | solution.py:132
  62.9 5.5 %collective-permute-start.10 = (bf16[560,128]{1,0:T(8,128)(2,1)S(1)}, bf16[560,128]{1,0:T(8,128)(2,1)S(1)}, u32[]{:S(2)}, u32[]{:S(2)}) collective-permute-start(bf16[560,128]{1,0:T(8,128)(2,1)S(1)} %get-tuple-element.64), channel_id=1, source_target_pairs={{0,128},{8,40},{16,144},{24,56},{32,160},{40,8},{48,176},{56,24},{... | collective-permute-start | bytes 430088 | tf_op jit(solution)/shard_map/ppermute | solution.py:132
  65.6 4.6 %collective-permute-start.11 = (bf16[560,128]{1,0:T(8,128)(2,1)S(1)}, bf16[560,128]{1,0:T(8,128)(2,1)S(1)}, u32[]{:S(2)}, u32[]{:S(2)}) collective-permute-start(bf16[560,128]{1,0:T(8,128)(2,1)S(1)} %get-tuple-element.65), channel_id=1, source_target_pairs={{0,192},{8,56},{16,208},{24,8},{32,224},{40,24},{48,240},{56,40},{... | collective-permute-start | bytes 430088 | tf_op jit(solution)/shard_map/ppermute | solution.py:132
  66.4 5.2 %collective-permute-start.9 = (bf16[560,128]{1,0:T(8,128)(2,1)S(1)}, bf16[560,128]{1,0:T(8,128)(2,1)S(1)}, u32[]{:S(2)}, u32[]{:S(2)}) collective-permute-start(bf16[560,128]{1,0:T(8,128)(2,1)S(1)} %get-tuple-element.63), channel_id=1, source_target_pairs={{0,64},{8,24},{16,80},{24,40},{32,96},{40,56},{48,112},{56,8},{64,... | collective-permute-start | bytes 430088 | tf_op jit(solution)/shard_map/ppermute | solution.py:132
  71.8 5.6 %collective-permute-start.13 = (bf16[560,128]{1,0:T(8,128)(2,1)S(1)}, bf16[560,128]{1,0:T(8,128)(2,1)S(1)}, u32[]{:S(2)}, u32[]{:S(2)}) collective-permute-start(bf16[560,128]{1,0:T(8,128)(2,1)S(1)} %get-tuple-element.66.a), channel_id=1, source_target_pairs={{0,128},{8,40},{16,144},{24,56},{32,160},{40,8},{48,176},{56,24},{... | collective-permute-start | bytes 430088 | tf_op jit(solution)/shard_map/ppermute | solution.py:132
  73.2 11.7 %collective-permute-start.12 = (bf16[560,128]{1,0:T(8,128)(2,1)S(1)}, bf16[560,128]{1,0:T(8,128)(2,1)S(1)}, u32[]{:S(2)}, u32[]{:S(2)}) collective-permute-start(bf16[560,128]{1,0:T(8,128)(2,1)S(1)} %get-tuple-element.66.a), channel_id=1, source_target_pairs={{0,64},{8,24},{16,80},{24,40},{32,96},{40,56},{48,112},{56,8},{64,... | collective-permute-start | bytes 430088 | tf_op jit(solution)/shard_map/ppermute | solution.py:132
  73.8 11.2 %collective-permute-start.14 = (bf16[560,128]{1,0:T(8,128)(2,1)S(1)}, bf16[560,128]{1,0:T(8,128)(2,1)S(1)}, u32[]{:S(2)}, u32[]{:S(2)}) collective-permute-start(bf16[560,128]{1,0:T(8,128)(2,1)S(1)} %get-tuple-element.66.a), channel_id=1, source_target_pairs={{0,192},{8,56},{16,208},{24,8},{32,224},{40,24},{48,240},{56,40},{... | collective-permute-start | bytes 430088 | tf_op jit(solution)/shard_map/ppermute | solution.py:132
  77.4 8.5 %collective-permute-start.15 = (bf16[560,128]{1,0:T(8,128)(2,1)S(1)}, bf16[560,128]{1,0:T(8,128)(2,1)S(1)}, u32[]{:S(2)}, u32[]{:S(2)}) collective-permute-start(bf16[560,128]{1,0:T(8,128)(2,1)S(1)} %collective-permute-done.13.c), channel_id=1, source_target_pairs={{0,8},{8,0},{1,9},{9,1},{2,10},{10,2},{3,11},{11,3},{4,12},{12,4},... | collective-permute-start | bytes 430088 | tf_op jit(solution)/shard_map/ppermute | solution.py:523
  85.9 7.1 %collective-permute-start.16 = (bf16[2,560,128]{2,1,0:T(8,128)(2,1)S(1)}, bf16[2,560,128]{2,1,0:T(8,128)(2,1)S(1)}, u32[]{:S(2)}, u32[]{:S(2)}) collective-permute-start(bf16[2,560,128]{2,1,0:T(8,128)(2,1)S(1)} %get-tuple-element.67.low), channel_id=1, source_target_pairs={{0,16},{8,72},{16,32},{24,88},{32,48},{40,104},{48,0},{56,120},{64... | collective-permute-start | bytes 860168 | tf_op jit(solution)/shard_map/ppermute | solution.py:132
  86.0 7.0 %collective-permute-start.19 = (bf16[2,560,128]{2,1,0:T(8,128)(2,1)S(1)}, bf16[2,560,128]{2,1,0:T(8,128)(2,1)S(1)}, u32[]{:S(2)}, u32[]{:S(2)}) collective-permute-start(bf16[2,560,128]{2,1,0:T(8,128)(2,1)S(1)} %get-tuple-element.68.high), channel_id=1, source_target_pairs={{0,48},{8,200},{16,0},{24,216},{32,16},{40,232},{48,32},{56,248},{... | collective-permute-start | bytes 860168 | tf_op jit(solution)/shard_map/ppermute | solution.py:132
  88.7 9.8 %collective-permute-start.17 = (bf16[2,560,128]{2,1,0:T(8,128)(2,1)S(1)}, bf16[2,560,128]{2,1,0:T(8,128)(2,1)S(1)}, u32[]{:S(2)}, u32[]{:S(2)}) collective-permute-start(bf16[2,560,128]{2,1,0:T(8,128)(2,1)S(1)} %get-tuple-element.68.high), channel_id=1, source_target_pairs={{0,16},{8,72},{16,32},{24,88},{32,48},{40,104},{48,0},{56,120},{64... | collective-permute-start | bytes 860168 | tf_op jit(solution)/shard_map/ppermute | solution.py:132
  88.7 12.4 %collective-permute-start.18 = (bf16[2,560,128]{2,1,0:T(8,128)(2,1)S(1)}, bf16[2,560,128]{2,1,0:T(8,128)(2,1)S(1)}, u32[]{:S(2)}, u32[]{:S(2)}) collective-permute-start(bf16[2,560,128]{2,1,0:T(8,128)(2,1)S(1)} %get-tuple-element.67.low), channel_id=1, source_target_pairs={{0,48},{8,200},{16,0},{24,216},{32,16},{40,232},{48,32},{56,248},{... | collective-permute-start | bytes 860168 | tf_op jit(solution)/shard_map/ppermute | solution.py:132
  93.0 10.6 %collective-permute-start.20 = (bf16[2,560,128]{2,1,0:T(8,128)(2,1)S(1)}, bf16[2,560,128]{2,1,0:T(8,128)(2,1)S(1)}, u32[]{:S(2)}, u32[]{:S(2)}) collective-permute-start(bf16[2,560,128]{2,1,0:T(8,128)(2,1)S(1)} %collective-permute-done.16.low), channel_id=1, source_target_pairs={{0,16},{8,72},{16,32},{24,88},{32,48},{40,104},{48,0},{56,120},{64... | collective-permute-start | bytes 860168 | tf_op jit(solution)/shard_map/ppermute | solution.py:132
  93.0 10.6 %collective-permute-start.21 = (bf16[2,560,128]{2,1,0:T(8,128)(2,1)S(1)}, bf16[2,560,128]{2,1,0:T(8,128)(2,1)S(1)}, u32[]{:S(2)}, u32[]{:S(2)}) collective-permute-start(bf16[2,560,128]{2,1,0:T(8,128)(2,1)S(1)} %collective-permute-done.19.high), channel_id=1, source_target_pairs={{0,48},{8,200},{16,0},{24,216},{32,16},{40,232},{48,32},{56,248},{... | collective-permute-start | bytes 860168 | tf_op jit(solution)/shard_map/ppermute | solution.py:132
  106.2 2.9 %collective-permute-start.22 = (f32[320,128]{1,0:T(8,128)S(1)}, f32[320,128]{1,0:T(8,128)S(1)}, u32[]{:S(2)}, u32[]{:S(2)}) collective-permute-start(f32[320,128]{1,0:T(8,128)S(1)} %get-tuple-element.84), channel_id=1, source_target_pairs={{0,8},{8,0},{1,9},{9,1},{2,10},{10,2},{3,11},{11,3},{4,12},{12,4},... | collective-permute-start | bytes 491528 | tf_op jit(solution)/shard_map/ppermute | solution.py:584
  109.1 18.2 %collective-permute-start.23 = (bf16[2,16,128,256]{3,2,1,0:T(8,128)(2,1)}, bf16[2,16,128,256]{3,2,1,0:T(8,128)(2,1)S(1)}, u32[]{:S(2)}, u32[]{:S(2)}) collective-permute-start(bf16[2,16,128,256]{3,2,1,0:T(8,128)(2,1)} %get-tuple-element.91), channel_id=1, source_target_pairs={{0,8},{8,0},{1,9},{9,1},{2,10},{10,2},{3,11},{11,3},{4,12},{12,4},... | collective-permute-start | bytes 6291464 | tf_op jit(solution)/shard_map/ppermute | solution.py:586
  110.2 15.4 %all-to-all-start.1 = ((bf16[8,40,384]{2,1,0:T(8,128)(2,1)}), bf16[8,40,384]{2,1,0:T(8,128)(2,1)S(1)}, u32[]{:S(2)}, u32[]{:S(2)}) async-start(bf16[8,40,384]{2,1,0:T(8,128)(2,1)} %bitcast.9), calls=%async_computation.1 | async-start | bytes 491520 | tf_op jit(solution)/shard_map/all_to_all | solution.py:412
